TPU v7x, 512 devices: a whole 4x8x8 slice. The times are simulated.
512 devices in a mesh: dom: 64 (over x, y, core), sub: 8 (over z).
Axes of the slice: x: 4, y: 8, z: 8, core: 2. Of those that a mesh axis runs over, the one named last changes fastest.
Arguments:
- inv_interior: bfloat16 [512, 80000], P(('dom', 'sub'))
- couple_if: bfloat16 [512, 160000], P(('dom', 'sub')), may hold values from -0.625 to 0.625
- couple_fi: bfloat16 [512, 160000], P(('dom', 'sub')), may hold values from -0.625 to 0.625
- face_face: bfloat16 [512, 320000], P(('dom', 'sub'))
- load_interior: float32 [4096, 100], P(('dom', 'sub')), may hold values from -6 to 6
- load_face: float32 [4096, 200], P(('dom', 'sub')), may hold values from -24 to 24
- jacobi_inverse: bfloat16 [12288, 2500], P(('dom', 'sub'))
- slot_face: int32 [4096, 4], P(('dom', 'sub')), may hold values from 0 to 24, as said below
- send_slot: int32 [512, 4, 2], P(('dom', 'sub')), may hold values from 0 to 32, as said below
- recv_face: int32 [512, 4, 2], P(('dom', 'sub')), may hold values from 0 to 24, as said below
- partner_sub: int32 [512, 8], P(('dom', 'sub')), may hold values from 0 to 7, as said below
- elem_count: int32 [512], P(('dom', 'sub')), may hold values from 4 to 8, as said below
Outputs:
- face_trace: float32 [12288, 50], P(('dom', 'sub'))
- interior_state: float32 [4096, 100], P(('dom', 'sub'))
- face_blocks: bfloat16 [12288, 2500], P(('dom', 'sub'))
Inputs may be any that keep to these rules, and one draw needn't show every extreme that they name: `slot_face`: for each element face: the index of its face among its own device's faces when that device owns it, else 24. Faces of elements at or past elem_count are 24. Every element face of a live element lies either here or in exactly one holder list; a face is met by one or two element faces. `send_slot`: holder lists of each device and group: element face positions 4 * e + k of this device, live rows first, 32 for empty rows; at most 2 live rows a list, and one list of some device has exactly 2. Row r matches row r of the owner's list, the owner of group g lying off(g) positions lower along dom, cyclically. `recv_face`: owner lists of each device and group: local face indices, live rows first, 24 for empty rows; the live rows equal in number those of the matching holder list, whose device lies off(g) positions higher along dom for group g. `partner_sub`: entry g is the sub index of the device's holder for group g; entry 4 + g that of its owner for group g. For each dom index and group, owners and holders are paired one to one by sub index; in group 0 no device is paired with itself. `elem_count`: live elements of each device; some device has 8.
All inputs are finite; a program needn't handle non-finite values.
Results may differ from a plain program's by a relative error of at most 0.0051.
Values sent between devices are 32-bit elements; how exact they have to be, the bound alone decides.
A program may use at most 64 MiB of HBM per device.

v0:
```python
import jax
import jax.numpy as jnp
from jax import lax
from jax.sharding import PartitionSpec as P

SWEEPS = 2


HIGH = lax.Precision.HIGHEST


def in_blocks(array, dim, length):
    before, after = (array.shape[:dim], array.shape[dim + 1 :])
    return jnp.moveaxis(array.reshape(*before, length, -1, *after), dim, 0)


def summed_on_arrival(array, axis, dim):
    tiles = in_blocks(array, dim, lax.axis_size(axis))
    arrived = lax.all_to_all(tiles, axis, split_axis=0, concat_axis=0, tiled=True)
    return arrived.sum(axis=0)


def from_behind(array, axis, by):
    length = lax.axis_size(axis)
    return lax.ppermute(array, axis, [(i, (i + by) % length) for i in range(length)])


def group_offset(group_index, dom_count):
    return [0, 1, dom_count // 2, dom_count - 1][group_index]


def pick_rows(values, index_table):
    padded = jnp.concatenate([values, jnp.zeros((1, values.shape[1]), values.dtype)], axis=0)
    return padded[index_table]


def spread_subs(picked, targets):
    sub_count = lax.axis_size("sub")
    select = (jnp.arange(sub_count, dtype=jnp.int32)[:, None] == targets[None, :]).astype(
        jnp.float32
    )
    return select[:, :, None, None] * picked[None]


def to_owners(values, send_slot, partner_sub):
    groups = send_slot.shape[1]
    dom_count = lax.axis_size("dom")
    spread = spread_subs(pick_rows(values, send_slot[0]), partner_sub[0, groups:])
    grouped = summed_on_arrival(spread, "sub", 0)[0]
    pieces = [grouped[0]]
    for group_index in range(1, groups):
        offset = group_offset(group_index, dom_count)
        pieces.append(from_behind(grouped[group_index], "dom", -offset))
    arrived = jnp.stack(pieces)
    return arrived.reshape(-1, values.shape[1])


def to_holders(values, recv_face, partner_sub):
    groups = recv_face.shape[1]
    dom_count = lax.axis_size("dom")
    spread = spread_subs(pick_rows(values, recv_face[0]), partner_sub[0, :groups])
    grouped = summed_on_arrival(spread, "sub", 0)[0]
    pieces = [grouped[0]]
    for group_index in range(1, groups):
        offset = group_offset(group_index, dom_count)
        pieces.append(from_behind(grouped[group_index], "dom", offset))
    arrived = jnp.stack(pieces)
    return arrived.reshape(-1, values.shape[1])


def per_device(
    inv_interior,
    couple_if,
    couple_fi,
    face_face,
    load_interior,
    load_face,
    jacobi_inverse,
    slot_face,
    send_slot,
    recv_face,
    partner_sub,
    elem_count,
):
    elements = load_interior.shape[0]
    interior = load_interior.shape[1]
    face_dof = load_face.shape[1] // 4
    face_width = 4 * face_dof
    face_count = jacobi_inverse.shape[0]
    slot_count = 4 * elements
    inverse_blocks = inv_interior.reshape(elements, interior, interior)
    couple_in = couple_if.reshape(elements, interior, face_width)
    couple_out = couple_fi.reshape(elements, face_width, interior)
    face_block = face_face.reshape(elements, face_width, face_width)
    living = (jnp.arange(elements, dtype=jnp.int32) < elem_count[0]).astype(jnp.float32)
    local_select = (
        jnp.arange(face_count, dtype=jnp.int32)[:, None] == slot_face.reshape(-1)[None, :]
    ).astype(jnp.float32)
    remote_select = (
        jnp.arange(face_count, dtype=jnp.int32)[:, None] == recv_face[0].reshape(-1)[None, :]
    ).astype(jnp.float32)
    holder_select = (
        jnp.arange(slot_count, dtype=jnp.int32)[:, None] == send_slot[0].reshape(-1)[None, :]
    ).astype(jnp.float32)

    def assemble(values):
        arrived = to_owners(values, send_slot, partner_sub)
        return jnp.dot(local_select, values, precision=HIGH) + jnp.dot(
            remote_select, arrived, precision=HIGH
        )

    def distribute(traces):
        arrived = to_holders(traces, recv_face, partner_sub)
        slot_traces = jnp.dot(local_select.T, traces, precision=HIGH) + jnp.dot(
            holder_select, arrived, precision=HIGH
        )
        return slot_traces.reshape(elements, face_width)

    interior_map = jnp.einsum(
        "eij,ejk->eik", inverse_blocks, couple_in, preferred_element_type=jnp.float32
    ).astype(jnp.bfloat16)
    product = jnp.einsum(
        "eij,ejk->eik", couple_out, interior_map, preferred_element_type=jnp.float32
    )
    condensed = ((face_block.astype(jnp.float32) - product) * living[:, None, None]).astype(
        jnp.bfloat16
    )
    interior_load = jnp.einsum(
        "eij,ej->ei", inverse_blocks.astype(jnp.float32), load_interior, precision=HIGH
    )
    face_load = (
        load_face
        - jnp.einsum("eij,ej->ei", couple_out.astype(jnp.float32), interior_load, precision=HIGH)
    ) * living[:, None]
    shaped = condensed.reshape(elements, 4, face_dof, 4, face_dof)
    blocks = jnp.stack([shaped[:, side_index, :, side_index, :] for side_index in range(4)], axis=1)
    blocks = blocks.reshape(slot_count, face_dof * face_dof).astype(jnp.float32)
    assembled = assemble(jnp.concatenate([blocks, face_load.reshape(slot_count, face_dof)], axis=1))
    face_blocks = assembled[:, : face_dof * face_dof].astype(jnp.bfloat16)
    face_rhs = assembled[:, face_dof * face_dof :]
    inverse = jacobi_inverse.astype(jnp.float32).reshape(face_count, face_dof, face_dof)
    traces = jnp.einsum("fij,fj->fi", inverse, face_rhs, precision=HIGH)
    condensed_wide = condensed.astype(jnp.float32)
    for sweep_index in range(SWEEPS):
        images = jnp.einsum("eij,ej->ei", condensed_wide, distribute(traces), precision=HIGH)
        residual = face_rhs - assemble(images.reshape(slot_count, face_dof))
        traces = traces + jnp.einsum("fij,fj->fi", inverse, residual, precision=HIGH)
    elem_traces = distribute(traces)
    interior_state = (
        interior_load
        - jnp.einsum("eij,ej->ei", interior_map.astype(jnp.float32), elem_traces, precision=HIGH)
    ) * living[:, None]
    return (traces, interior_state, face_blocks)


def solution(mesh):
    placed = (
        P(("dom", "sub"), None),
        P(("dom", "sub"), None),
        P(("dom", "sub"), None),
        P(("dom", "sub"), None),
        P(("dom", "sub"), None),
        P(("dom", "sub"), None),
        P(("dom", "sub"), None),
        P(("dom", "sub"), None),
        P(("dom", "sub"), None, None),
        P(("dom", "sub"), None, None),
        P(("dom", "sub"), None),
        P(("dom", "sub")),
    )
    return jax.shard_map(
        per_device,
        mesh=mesh,
        in_specs=placed,
        out_specs=(P(("dom", "sub"), None), P(("dom", "sub"), None), P(("dom", "sub"), None)),
        check_vma=False,
    )
```

profile of v0, /device:TPU:1, one launch (start us, length us, event | category | flops | bytes accessed | tf_op | source)
XLA Modules:
  0.0 231.0 jit_solution(11287364308653534871)
XLA Ops:
  0.7 7.6 %reduce.9 = bf16[160000]{0:T(1024)(128)(2,1)S(1)} reduce(bf16[1,160000]{1,0:T(2,128)(2,1)} %param.14, bf16[]{:T(256)} %constant.35), dimensions={0}, to_apply=%param.14.reduce_sub_computation | reduce | bytes 640002 | tf_op args[2]
  8.3 1.6 reshape.254
  9.9 0.9 reduce.7
  12.2 0.7 fusion.23
  13.1 13.0 %convert_reduce_fusion = f32[320000]{0:T(1024)S(1)} fusion(bf16[1,320000]{1,0:T(2,128)(2,1)} %param.15), kind=kLoop, calls=%fused_computation.10 | loop fusion | flops 320000 | bytes 1920000 | tf_op jit(solution)/shard_map/convert_element_type | solution.py:125
  26.1 3.6 %reshape.269 = f32[8,200,200]{2,1,0:T(8,128)} reshape(f32[320000]{0:T(1024)S(1)} %convert_reduce_fusion) | data formatting | bytes 2560000 | tf_op jit(solution)/shard_map/convert_element_type | solution.py:125
  29.7 1.9 copy.51
  31.6 6.8 %reduce.8 = bf16[160000]{0:T(1024)(128)(2,1)S(1)} reduce(bf16[1,160000]{1,0:T(2,128)(2,1)S(1)} %copy-done.1, bf16[]{:T(256)} %constant.35), dimensions={0}, to_apply=%param.13.reduce_sub_computation | reduce | bytes 640002 | tf_op args[1]
  38.4 0.8 reshape.253
  40.1 0.9 reshape.255
  41.0 1.5 fusion.27
  42.4 1.1 copy.93
  46.0 1.1 broadcast_multiply_fusion
  47.0 10.9 %all-to-all-start = ((f32[8,1,4,2,2550]{4,3,2,1,0:T(2,128)}), f32[8,1,4,2,2550]{4,3,2,1,0:T(2,128)S(1)}, u32[]{:S(2)}, u32[]{:S(2)}) async-start(f32[8,1,4,2,2550]{4,3,2,1,0:T(2,128)} %broadcast_multiply_fusion), calls=%async_computation | async-start | bytes 1310720 | tf_op jit(solution)/shard_map/all_to_all | solution.py:19
  58.5 20.1 %all-to-all-done = f32[8,1,4,2,2550]{4,3,2,1,0:T(2,128)S(1)} async-done(((f32[8,1,4,2,2550]{4,3,2,1,0:T(2,128)}), f32[8,1,4,2,2550]{4,3,2,1,0:T(2,128)S(1)}, u32[]{:S(2)}, u32[]{:S(2)}) %all-to-all-start) | async-done | bytes 652832 | tf_op jit(solution)/shard_map/all_to_all | solution.py:19
  79.0 3.6 %collective-permute-start.2 = (f32[2,2550]{1,0:T(2,128)S(1)}, f32[2,2550]{1,0:T(2,128)S(1)}, u32[]{:S(2)}, u32[]{:S(2)}) collective-permute-start(f32[2,2550]{1,0:T(2,128)S(1)} %get-tuple-element.8), channel_id=1, source_target_pairs={{0,8},{8,16},{16,24},{24,32},{32,40},{40,48},{48,56},{56,64},{64,7... | collective-permute-start | bytes 61208 | tf_op jit(solution)/shard_map/ppermute | solution.py:25
  82.6 4.7 %collective-permute-start.1 = (f32[2,2550]{1,0:T(2,128)S(1)}, f32[2,2550]{1,0:T(2,128)S(1)}, u32[]{:S(2)}, u32[]{:S(2)}) collective-permute-start(f32[2,2550]{1,0:T(2,128)S(1)} %get-tuple-element.9), channel_id=1, source_target_pairs={{0,256},{8,264},{16,272},{24,280},{32,288},{40,296},{48,304},{56,3... | collective-permute-start | bytes 61208 | tf_op jit(solution)/shard_map/ppermute | solution.py:25
  87.2 1.9 collective-permute-start
  89.7 2.6 %collective-permute-done = f32[2,2550]{1,0:T(2,128)S(1)} collective-permute-done((f32[2,2550]{1,0:T(2,128)S(1)}, f32[2,2550]{1,0:T(2,128)S(1)}, u32[]{:S(2)}, u32[]{:S(2)}) %collective-permute-start) | collective-permute-done | bytes 20432 | tf_op jit(solution)/shard_map/ppermute | solution.py:25
  94.1 0.7 reshape.351
  94.8 3.3 %all-to-all-start.1 = ((f32[8,1,400]{2,1,0:T(1,128)}), f32[8,1,400]{2,1,0:T(1,128)S(1)}, u32[]{:S(2)}, u32[]{:S(2)}) async-start(f32[8,1,400]{2,1,0:T(1,128)} %reshape.351), calls=%async_computation.1 | async-start | bytes 32768 | tf_op jit(solution)/shard_map/all_to_all | solution.py:19
  98.3 6.4 %all-to-all-done.1 = f32[8,1,400]{2,1,0:T(1,128)S(1)} async-done(((f32[8,1,400]{2,1,0:T(1,128)}), f32[8,1,400]{2,1,0:T(1,128)S(1)}, u32[]{:S(2)}, u32[]{:S(2)}) %all-to-all-start.1) | async-done | bytes 12832 | tf_op jit(solution)/shard_map/all_to_all | solution.py:19
  106.0 4.6 %collective-permute-start.5 = (f32[2,50]{1,0:T(2,128)S(1)}, f32[2,50]{1,0:T(2,128)S(1)}, u32[]{:S(2)}, u32[]{:S(2)}) collective-permute-start(f32[2,50]{1,0:T(2,128)S(1)} %get-tuple-element.28), channel_id=1, source_target_pairs={{0,504},{8,0},{16,8},{24,16},{32,24},{40,32},{48,40},{56,48},{64,5... | collective-permute-start | bytes 1208 | tf_op jit(solution)/shard_map/ppermute | solution.py:25
  110.7 2.4 %collective-permute-start.4 = (f32[2,50]{1,0:T(2,128)S(1)}, f32[2,50]{1,0:T(2,128)S(1)}, u32[]{:S(2)}, u32[]{:S(2)}) collective-permute-start(f32[2,50]{1,0:T(2,128)S(1)} %get-tuple-element.29), channel_id=1, source_target_pairs={{0,256},{8,264},{16,272},{24,280},{32,288},{40,296},{48,304},{56,3... | collective-permute-start | bytes 1208 | tf_op jit(solution)/shard_map/ppermute | solution.py:25
  113.0 1.9 collective-permute-start.3
  115.2 1.3 collective-permute-done.4
  116.5 2.6 %collective-permute-done.3 = f32[2,50]{1,0:T(2,128)S(1)} collective-permute-done((f32[2,50]{1,0:T(2,128)S(1)}, f32[2,50]{1,0:T(2,128)S(1)}, u32[]{:S(2)}, u32[]{:S(2)}) %collective-permute-start.3) | collective-permute-done | bytes 432 | tf_op jit(solution)/shard_map/ppermute | solution.py:25
  120.6 9.0 %all_to_all.30 = f32[8,1,400]{2,1,0:T(1,128)S(1)} all-to-all(f32[8,1,400]{2,1,0:T(1,128)S(1)} %reshape.353), channel_id=1, replica_groups=mesh['dom'=64,'sub'=8] {'sub'}, dimensions={0} | all-to-all | bytes 25600 | tf_op jit(solution)/shard_map/all_to_all | solution.py:19
  130.4 2.0 collective-permute-start.8
  132.4 5.1 %collective-permute-start.7 = (f32[2,50]{1,0:T(2,128)S(1)}, f32[2,50]{1,0:T(2,128)S(1)}, u32[]{:S(2)}, u32[]{:S(2)}) collective-permute-start(f32[2,50]{1,0:T(2,128)S(1)} %get-tuple-element.25), channel_id=1, source_target_pairs={{0,256},{8,264},{16,272},{24,280},{32,288},{40,296},{48,304},{56,3... | collective-permute-start | bytes 1208 | tf_op jit(solution)/shard_map/ppermute | solution.py:25
  137.5 7.8 %collective-permute-start.6 = (f32[2,50]{1,0:T(2,128)S(1)}, f32[2,50]{1,0:T(2,128)S(1)}, u32[]{:S(2)}, u32[]{:S(2)}) collective-permute-start(f32[2,50]{1,0:T(2,128)S(1)} %get-tuple-element.26), channel_id=1, source_target_pairs={{0,504},{8,0},{16,8},{24,16},{32,24},{40,32},{48,40},{56,48},{64,5... | collective-permute-start | bytes 1208 | tf_op jit(solution)/shard_map/ppermute | solution.py:25
  147.7 9.0 %all_to_all.31 = f32[8,1,400]{2,1,0:T(1,128)S(1)} all-to-all(f32[8,1,400]{2,1,0:T(1,128)S(1)} %reshape.355), channel_id=1, replica_groups=mesh['dom'=64,'sub'=8] {'sub'}, dimensions={0} | all-to-all | bytes 25600 | tf_op jit(solution)/shard_map/all_to_all | solution.py:19
  157.5 7.7 %collective-permute-start.11 = (f32[2,50]{1,0:T(2,128)S(1)}, f32[2,50]{1,0:T(2,128)S(1)}, u32[]{:S(2)}, u32[]{:S(2)}) collective-permute-start(f32[2,50]{1,0:T(2,128)S(1)} %get-tuple-element.20), channel_id=1, source_target_pairs={{0,504},{8,0},{16,8},{24,16},{32,24},{40,32},{48,40},{56,48},{64,5... | collective-permute-start | bytes 1208 | tf_op jit(solution)/shard_map/ppermute | solution.py:25
  165.2 2.9 %collective-permute-start.10 = (f32[2,50]{1,0:T(2,128)S(1)}, f32[2,50]{1,0:T(2,128)S(1)}, u32[]{:S(2)}, u32[]{:S(2)}) collective-permute-start(f32[2,50]{1,0:T(2,128)S(1)} %get-tuple-element.21), channel_id=1, source_target_pairs={{0,256},{8,264},{16,272},{24,280},{32,288},{40,296},{48,304},{56,3... | collective-permute-start | bytes 1208 | tf_op jit(solution)/shard_map/ppermute | solution.py:25
  168.1 1.9 collective-permute-start.9
  170.2 0.8 collective-permute-done.10
  171.1 2.5 %collective-permute-done.9 = f32[2,50]{1,0:T(2,128)S(1)} collective-permute-done((f32[2,50]{1,0:T(2,128)S(1)}, f32[2,50]{1,0:T(2,128)S(1)}, u32[]{:S(2)}, u32[]{:S(2)}) %collective-permute-start.9) | collective-permute-done | bytes 432 | tf_op jit(solution)/shard_map/ppermute | solution.py:25
  175.1 9.0 %all_to_all.32 = f32[8,1,400]{2,1,0:T(1,128)S(1)} all-to-all(f32[8,1,400]{2,1,0:T(1,128)S(1)} %reshape.357), channel_id=1, replica_groups=mesh['dom'=64,'sub'=8] {'sub'}, dimensions={0} | all-to-all | bytes 25600 | tf_op jit(solution)/shard_map/all_to_all | solution.py:19
  185.0 2.5 %collective-permute-start.14 = (f32[2,50]{1,0:T(2,128)S(1)}, f32[2,50]{1,0:T(2,128)S(1)}, u32[]{:S(2)}, u32[]{:S(2)}) collective-permute-start(f32[2,50]{1,0:T(2,128)S(1)} %get-tuple-element.16), channel_id=1, source_target_pairs={{0,8},{8,16},{16,24},{24,32},{32,40},{40,48},{48,56},{56,64},{64,7... | collective-permute-start | bytes 1208 | tf_op jit(solution)/shard_map/ppermute | solution.py:25
  187.4 4.6 %collective-permute-start.13 = (f32[2,50]{1,0:T(2,128)S(1)}, f32[2,50]{1,0:T(2,128)S(1)}, u32[]{:S(2)}, u32[]{:S(2)}) collective-permute-start(f32[2,50]{1,0:T(2,128)S(1)} %get-tuple-element.17), channel_id=1, source_target_pairs={{0,256},{8,264},{16,272},{24,280},{32,288},{40,296},{48,304},{56,3... | collective-permute-start | bytes 1208 | tf_op jit(solution)/shard_map/ppermute | solution.py:25
  192.1 7.8 %collective-permute-start.12 = (f32[2,50]{1,0:T(2,128)S(1)}, f32[2,50]{1,0:T(2,128)S(1)}, u32[]{:S(2)}, u32[]{:S(2)}) collective-permute-start(f32[2,50]{1,0:T(2,128)S(1)} %get-tuple-element.18), channel_id=1, source_target_pairs={{0,504},{8,0},{16,8},{24,16},{32,24},{40,32},{48,40},{56,48},{64,5... | collective-permute-start | bytes 1208 | tf_op jit(solution)/shard_map/ppermute | solution.py:25
  202.8 3.3 %all-to-all-start.5 = ((f32[8,1,400]{2,1,0:T(1,128)}), f32[8,1,400]{2,1,0:T(1,128)S(1)}, u32[]{:S(2)}, u32[]{:S(2)}) async-start(f32[8,1,400]{2,1,0:T(1,128)} %reshape.359), calls=%async_computation.5 | async-start | bytes 32768 | tf_op jit(solution)/shard_map/all_to_all | solution.py:19
  206.8 5.9 %all-to-all-done.5 = f32[8,1,400]{2,1,0:T(1,128)S(1)} async-done(((f32[8,1,400]{2,1,0:T(1,128)}), f32[8,1,400]{2,1,0:T(1,128)S(1)}, u32[]{:S(2)}, u32[]{:S(2)}) %all-to-all-start.5) | async-done | bytes 12832 | tf_op jit(solution)/shard_map/all_to_all | solution.py:19
  213.6 7.7 %collective-permute-start.17 = (f32[2,50]{1,0:T(2,128)S(1)}, f32[2,50]{1,0:T(2,128)S(1)}, u32[]{:S(2)}, u32[]{:S(2)}) collective-permute-start(f32[2,50]{1,0:T(2,128)S(1)} %get-tuple-element.12), channel_id=1, source_target_pairs={{0,504},{8,0},{16,8},{24,16},{32,24},{40,32},{48,40},{56,48},{64,5... | collective-permute-start | bytes 1208 | tf_op jit(solution)/shard_map/ppermute | solution.py:25
  221.3 2.9 %collective-permute-start.16 = (f32[2,50]{1,0:T(2,128)S(1)}, f32[2,50]{1,0:T(2,128)S(1)}, u32[]{:S(2)}, u32[]{:S(2)}) collective-permute-start(f32[2,50]{1,0:T(2,128)S(1)} %get-tuple-element.13), channel_id=1, source_target_pairs={{0,256},{8,264},{16,272},{24,280},{32,288},{40,296},{48,304},{56,3... | collective-permute-start | bytes 1208 | tf_op jit(solution)/shard_map/ppermute | solution.py:25
  224.1 1.9 collective-permute-start.15
  226.3 0.8 collective-permute-done.16
  227.1 2.5 %collective-permute-done.15 = f32[2,50]{1,0:T(2,128)S(1)} collective-permute-done((f32[2,50]{1,0:T(2,128)S(1)}, f32[2,50]{1,0:T(2,128)S(1)}, u32[]{:S(2)}, u32[]{:S(2)}) %collective-permute-start.15) | collective-permute-done | bytes 432 | tf_op jit(solution)/shard_map/ppermute | solution.py:25
  (145 shorter events, 23.0 us)
Async XLA Ops:
  0.6 11.2 %copy-start = (f32[8,100]{1,0:T(8,128)S(1)}, f32[8,100]{1,0:T(8,128)}, u32[]{:S(2)}) copy-start(f32[8,100]{1,0:T(8,128)} %param.16) | copy-start | bytes 9604
  0.6 9.2 %copy-start.2 = (bf16[1,80000]{1,0:T(2,128)(2,1)S(1)}, bf16[1,80000]{1,0:T(2,128)(2,1)}, u32[]{:S(2)}) copy-start(bf16[1,80000]{1,0:T(2,128)(2,1)} %param.12) | copy-start | bytes 480004
  0.7 12.3 %copy-start.5 = (f32[8,200]{1,0:T(8,128)S(1)}, f32[8,200]{1,0:T(8,128)}, u32[]{:S(2)}) copy-start(f32[8,200]{1,0:T(8,128)} %param.17) | copy-start | bytes 19204
  29.7 1.9 copy-start.1
  44.2 0.7 copy-start.7
  44.4 1.5 copy-start.9
  45.2 12.7 %copy-start.8 = (s32[8,4]{0,1:T(4,128)S(1)}, s32[8,4]{0,1:T(4,128)}, u32[]{:S(2)}) copy-start(s32[8,4]{0,1:T(4,128)} %param.19) | copy-start | bytes 388
  45.2 12.8 %copy-start.6 = (s32[1,4,2]{1,2,0:T(2,128)S(1)}, s32[1,4,2]{1,2,0:T(2,128)}, u32[]{:S(2)}) copy-start(s32[1,4,2]{1,2,0:T(2,128)} %param.21) | copy-start | bytes 100
  46.0 43.4 %copy-start.3 = (bf16[24,2500]{1,0:T(8,128)(2,1)S(1)}, bf16[24,2500]{1,0:T(8,128)(2,1)}, u32[]{:S(2)}) copy-start(bf16[24,2500]{1,0:T(8,128)(2,1)} %param.18) | copy-start | bytes 360004
  47.0 31.6 %all-to-all-start = ((f32[8,1,4,2,2550]{4,3,2,1,0:T(2,128)}), f32[8,1,4,2,2550]{4,3,2,1,0:T(2,128)S(1)}, u32[]{:S(2)}, u32[]{:S(2)}) async-start(f32[8,1,4,2,2550]{4,3,2,1,0:T(2,128)} %broadcast_multiply_fusion), calls=%async_computation | async-start | bytes 1310720 | tf_op jit(solution)/shard_map/all_to_all | solution.py:19
  79.0 10.7 %collective-permute-start.2 = (f32[2,2550]{1,0:T(2,128)S(1)}, f32[2,2550]{1,0:T(2,128)S(1)}, u32[]{:S(2)}, u32[]{:S(2)}) collective-permute-start(f32[2,2550]{1,0:T(2,128)S(1)} %get-tuple-element.8), channel_id=1, source_target_pairs={{0,8},{8,16},{16,24},{24,32},{32,40},{40,48},{48,56},{56,64},{64,7... | collective-permute-start | bytes 61208 | tf_op jit(solution)/shard_map/ppermute | solution.py:25
  82.6 7.1 %collective-permute-start.1 = (f32[2,2550]{1,0:T(2,128)S(1)}, f32[2,2550]{1,0:T(2,128)S(1)}, u32[]{:S(2)}, u32[]{:S(2)}) collective-permute-start(f32[2,2550]{1,0:T(2,128)S(1)} %get-tuple-element.9), channel_id=1, source_target_pairs={{0,256},{8,264},{16,272},{24,280},{32,288},{40,296},{48,304},{56,3... | collective-permute-start | bytes 61208 | tf_op jit(solution)/shard_map/ppermute | solution.py:25
  87.2 5.1 %collective-permute-start = (f32[2,2550]{1,0:T(2,128)S(1)}, f32[2,2550]{1,0:T(2,128)S(1)}, u32[]{:S(2)}, u32[]{:S(2)}) collective-permute-start(f32[2,2550]{1,0:T(2,128)S(1)} %get-tuple-element.10), channel_id=1, source_target_pairs={{0,504},{8,0},{16,8},{24,16},{32,24},{40,32},{48,40},{56,48},{64,5... | collective-permute-start | bytes 61208 | tf_op jit(solution)/shard_map/ppermute | solution.py:25
  94.8 9.9 %all-to-all-start.1 = ((f32[8,1,400]{2,1,0:T(1,128)}), f32[8,1,400]{2,1,0:T(1,128)S(1)}, u32[]{:S(2)}, u32[]{:S(2)}) async-start(f32[8,1,400]{2,1,0:T(1,128)} %reshape.351), calls=%async_computation.1 | async-start | bytes 32768 | tf_op jit(solution)/shard_map/all_to_all | solution.py:19
  106.0 9.1 %collective-permute-start.5 = (f32[2,50]{1,0:T(2,128)S(1)}, f32[2,50]{1,0:T(2,128)S(1)}, u32[]{:S(2)}, u32[]{:S(2)}) collective-permute-start(f32[2,50]{1,0:T(2,128)S(1)} %get-tuple-element.28), channel_id=1, source_target_pairs={{0,504},{8,0},{16,8},{24,16},{32,24},{40,32},{48,40},{56,48},{64,5... | collective-permute-start | bytes 1208 | tf_op jit(solution)/shard_map/ppermute | solution.py:25
  110.7 5.8 %collective-permute-start.4 = (f32[2,50]{1,0:T(2,128)S(1)}, f32[2,50]{1,0:T(2,128)S(1)}, u32[]{:S(2)}, u32[]{:S(2)}) collective-permute-start(f32[2,50]{1,0:T(2,128)S(1)} %get-tuple-element.29), channel_id=1, source_target_pairs={{0,256},{8,264},{16,272},{24,280},{32,288},{40,296},{48,304},{56,3... | collective-permute-start | bytes 1208 | tf_op jit(solution)/shard_map/ppermute | solution.py:25
  113.0 6.0 %collective-permute-start.3 = (f32[2,50]{1,0:T(2,128)S(1)}, f32[2,50]{1,0:T(2,128)S(1)}, u32[]{:S(2)}, u32[]{:S(2)}) collective-permute-start(f32[2,50]{1,0:T(2,128)S(1)} %get-tuple-element.30), channel_id=1, source_target_pairs={{0,8},{8,16},{16,24},{24,32},{32,40},{40,48},{48,56},{56,64},{64,7... | collective-permute-start | bytes 1208 | tf_op jit(solution)/shard_map/ppermute | solution.py:25
  130.4 15.0 %collective-permute-start.8 = (f32[2,50]{1,0:T(2,128)S(1)}, f32[2,50]{1,0:T(2,128)S(1)}, u32[]{:S(2)}, u32[]{:S(2)}) collective-permute-start(f32[2,50]{1,0:T(2,128)S(1)} %get-tuple-element.24), channel_id=1, source_target_pairs={{0,8},{8,16},{16,24},{24,32},{32,40},{40,48},{48,56},{56,64},{64,7... | collective-permute-start | bytes 1208 | tf_op jit(solution)/shard_map/ppermute | solution.py:25
  132.4 13.1 %collective-permute-start.7 = (f32[2,50]{1,0:T(2,128)S(1)}, f32[2,50]{1,0:T(2,128)S(1)}, u32[]{:S(2)}, u32[]{:S(2)}) collective-permute-start(f32[2,50]{1,0:T(2,128)S(1)} %get-tuple-element.25), channel_id=1, source_target_pairs={{0,256},{8,264},{16,272},{24,280},{32,288},{40,296},{48,304},{56,3... | collective-permute-start | bytes 1208 | tf_op jit(solution)/shard_map/ppermute | solution.py:25
  137.5 8.6 %collective-permute-start.6 = (f32[2,50]{1,0:T(2,128)S(1)}, f32[2,50]{1,0:T(2,128)S(1)}, u32[]{:S(2)}, u32[]{:S(2)}) collective-permute-start(f32[2,50]{1,0:T(2,128)S(1)} %get-tuple-element.26), channel_id=1, source_target_pairs={{0,504},{8,0},{16,8},{24,16},{32,24},{40,32},{48,40},{56,48},{64,5... | collective-permute-start | bytes 1208 | tf_op jit(solution)/shard_map/ppermute | solution.py:25
  157.5 12.7 %collective-permute-start.11 = (f32[2,50]{1,0:T(2,128)S(1)}, f32[2,50]{1,0:T(2,128)S(1)}, u32[]{:S(2)}, u32[]{:S(2)}) collective-permute-start(f32[2,50]{1,0:T(2,128)S(1)} %get-tuple-element.20), channel_id=1, source_target_pairs={{0,504},{8,0},{16,8},{24,16},{32,24},{40,32},{48,40},{56,48},{64,5... | collective-permute-start | bytes 1208 | tf_op jit(solution)/shard_map/ppermute | solution.py:25
  165.2 5.8 %collective-permute-start.10 = (f32[2,50]{1,0:T(2,128)S(1)}, f32[2,50]{1,0:T(2,128)S(1)}, u32[]{:S(2)}, u32[]{:S(2)}) collective-permute-start(f32[2,50]{1,0:T(2,128)S(1)} %get-tuple-element.21), channel_id=1, source_target_pairs={{0,256},{8,264},{16,272},{24,280},{32,288},{40,296},{48,304},{56,3... | collective-permute-start | bytes 1208 | tf_op jit(solution)/shard_map/ppermute | solution.py:25
  168.1 5.5 %collective-permute-start.9 = (f32[2,50]{1,0:T(2,128)S(1)}, f32[2,50]{1,0:T(2,128)S(1)}, u32[]{:S(2)}, u32[]{:S(2)}) collective-permute-start(f32[2,50]{1,0:T(2,128)S(1)} %get-tuple-element.22), channel_id=1, source_target_pairs={{0,8},{8,16},{16,24},{24,32},{32,40},{40,48},{48,56},{56,64},{64,7... | collective-permute-start | bytes 1208 | tf_op jit(solution)/shard_map/ppermute | solution.py:25
  185.0 15.0 %collective-permute-start.14 = (f32[2,50]{1,0:T(2,128)S(1)}, f32[2,50]{1,0:T(2,128)S(1)}, u32[]{:S(2)}, u32[]{:S(2)}) collective-permute-start(f32[2,50]{1,0:T(2,128)S(1)} %get-tuple-element.16), channel_id=1, source_target_pairs={{0,8},{8,16},{16,24},{24,32},{32,40},{40,48},{48,56},{56,64},{64,7... | collective-permute-start | bytes 1208 | tf_op jit(solution)/shard_map/ppermute | solution.py:25
  187.4 12.5 %collective-permute-start.13 = (f32[2,50]{1,0:T(2,128)S(1)}, f32[2,50]{1,0:T(2,128)S(1)}, u32[]{:S(2)}, u32[]{:S(2)}) collective-permute-start(f32[2,50]{1,0:T(2,128)S(1)} %get-tuple-element.17), channel_id=1, source_target_pairs={{0,256},{8,264},{16,272},{24,280},{32,288},{40,296},{48,304},{56,3... | collective-permute-start | bytes 1208 | tf_op jit(solution)/shard_map/ppermute | solution.py:25
  192.1 8.6 %collective-permute-start.12 = (f32[2,50]{1,0:T(2,128)S(1)}, f32[2,50]{1,0:T(2,128)S(1)}, u32[]{:S(2)}, u32[]{:S(2)}) collective-permute-start(f32[2,50]{1,0:T(2,128)S(1)} %get-tuple-element.18), channel_id=1, source_target_pairs={{0,504},{8,0},{16,8},{24,16},{32,24},{40,32},{48,40},{56,48},{64,5... | collective-permute-start | bytes 1208 | tf_op jit(solution)/shard_map/ppermute | solution.py:25
  201.4 29.5 %copy-start.4 = (f32[24,50]{1,0:T(8,128)}, f32[24,50]{1,0:T(8,128)S(1)}, u32[]{:S(2)}) copy-start(f32[24,50]{1,0:T(8,128)S(1)} %add.68) | copy-start | bytes 14404
  202.8 9.9 %all-to-all-start.5 = ((f32[8,1,400]{2,1,0:T(1,128)}), f32[8,1,400]{2,1,0:T(1,128)S(1)}, u32[]{:S(2)}, u32[]{:S(2)}) async-start(f32[8,1,400]{2,1,0:T(1,128)} %reshape.359), calls=%async_computation.5 | async-start | bytes 32768 | tf_op jit(solution)/shard_map/all_to_all | solution.py:19
  213.6 12.7 %collective-permute-start.17 = (f32[2,50]{1,0:T(2,128)S(1)}, f32[2,50]{1,0:T(2,128)S(1)}, u32[]{:S(2)}, u32[]{:S(2)}) collective-permute-start(f32[2,50]{1,0:T(2,128)S(1)} %get-tuple-element.12), channel_id=1, source_target_pairs={{0,504},{8,0},{16,8},{24,16},{32,24},{40,32},{48,40},{56,48},{64,5... | collective-permute-start | bytes 1208 | tf_op jit(solution)/shard_map/ppermute | solution.py:25
  221.3 5.8 %collective-permute-start.16 = (f32[2,50]{1,0:T(2,128)S(1)}, f32[2,50]{1,0:T(2,128)S(1)}, u32[]{:S(2)}, u32[]{:S(2)}) collective-permute-start(f32[2,50]{1,0:T(2,128)S(1)} %get-tuple-element.13), channel_id=1, source_target_pairs={{0,256},{8,264},{16,272},{24,280},{32,288},{40,296},{48,304},{56,3... | collective-permute-start | bytes 1208 | tf_op jit(solution)/shard_map/ppermute | solution.py:25
  224.1 5.5 %collective-permute-start.15 = (f32[2,50]{1,0:T(2,128)S(1)}, f32[2,50]{1,0:T(2,128)S(1)}, u32[]{:S(2)}, u32[]{:S(2)}) collective-permute-start(f32[2,50]{1,0:T(2,128)S(1)} %get-tuple-element.14), channel_id=1, source_target_pairs={{0,8},{8,16},{16,24},{24,32},{32,40},{40,48},{48,56},{56,64},{64,7... | collective-permute-start | bytes 1208 | tf_op jit(solution)/shard_map/ppermute | solution.py:25
where the time goes:
time: 235 us; the launch traced here: 231 us
  starting transfers between devices  91.2 us (39%)
  waiting for transfers between devices  46.9 us (20%)
  other arithmetic  34.9 us (15%)
  blocking collectives  26.9 us (11%)
  local copies, waits for them, and re-layouts  21.7 us (9%)
  matrix products  7.21 us (3%)
    ppermute x18, starting transfers between devices, from_behind(): lax.ppermute(array, axis, [(i, (i + by) % length) for i in range(length)])  73.7 us
    all_to_all x3, waiting for transfers between devices, summed_on_arrival(): lax.all_to_all(tiles, axis, split_axis=0, concat_axis=0, tiled=True)  32.4 us
    all_to_all x3, blocking collectives, summed_on_arrival(): lax.all_to_all(tiles, axis, split_axis=0, concat_axis=0, tiled=True)  26.9 us
    all_to_all x3, starting transfers between devices, summed_on_arrival(): lax.all_to_all(tiles, axis, split_axis=0, concat_axis=0, tiled=True)  17.5 us
    unnamed x3, other arithmetic  15.4 us
    ppermute x18, waiting for transfers between devices, from_behind(): lax.ppermute(array, axis, [(i, (i + by) % length) for i in range(length)])  14.5 us
    convert_element_type x1, other arithmetic, per_device(): face_block.astype(jnp.float32) - product  13 us
    convert_element_type x2, local copies, waits for them, and re-layouts, per_device(): face_block.astype(jnp.float32) - product  5.44 us
  transfers between devices with their start and end apart: 21, of which 12 were waited for; matrix products, arithmetic and copies ran while one was open for 1% of the time, Pallas kernels for 0%

commit v1 on v0

v1 whole, which is shorter than its diff:
```python
import functools

import jax
import jax.numpy as jnp
from jax import lax
from jax.experimental import pallas as pl
from jax.experimental.pallas import tpu as pltpu
from jax.sharding import PartitionSpec as P

HIGH = lax.Precision.HIGHEST
SWEEPS = 2
GROUPS = 4
DOF = 50
CHUNKS = 5
F32, BF16 = jnp.float32, jnp.bfloat16


def group_offset(group, doms):
    return [0, 1, doms // 2, doms - 1][group]


def split_dot(left, right):
    high = right.astype(BF16)
    low = (right - high.astype(F32)).astype(BF16)
    return jnp.dot(left, high, preferred_element_type=F32) + jnp.dot(
        left, low, preferred_element_type=F32
    )


def exchange_kernel(
    doms, subs,
    select_ref, partner_ref, condensed_ref, imap_ref, iload_ref, fload_ref, jac_ref, blocks_ref, living_ref,
    trace_ref, state_ref, faces_ref,
    jflat, jrows, sbuf, rbuf, sbig, rbig, send_sem, recv_sem, bsend_sem, brecv_sem,
):
    dom, sub = lax.axis_index("dom"), lax.axis_index("sub")
    offsets = [group_offset(g, doms) for g in range(GROUPS)]
    for phase in range(6):
        rbuf[phase] = jnp.zeros(rbuf.shape[1:], F32)
    barrier = pltpu.get_barrier_semaphore()

    def greet(step, carry):
        for g in range(GROUPS):
            other = lax.rem(sub + step, subs)
            target = lax.rem(dom + offsets[g], doms)

            def signal():
                pl.semaphore_signal(barrier, inc=1, device_id=(target, other), device_id_type=pl.DeviceIdType.MESH)

            if g == 0:
                pl.when(step > 0)(signal)
            else:
                signal()
        return carry

    lax.fori_loop(0, subs, greet, 0)

    jflat[:, 0:2500] = jac_ref[...].astype(F32)
    jflat[:, 2500:2688] = jnp.zeros((24, 188), F32)
    for i in range(DOF):
        start = DOF * i
        tile = start // 128 * 128
        window = jflat[:, tile : tile + 256] if tile + 256 <= 2688 else jflat[:, 2432:2688]
        base = tile if tile + 256 <= 2688 else 2432
        jrows[i] = pltpu.roll(window, 256 - (start - base), 1)[:, 0:128]

    lane24 = lax.broadcasted_iota(jnp.int32, (24, 128), 1)
    row8 = lax.broadcasted_iota(jnp.int32, (8, 200), 0)

    def jacobi(vector):
        total = jnp.zeros((24, 128), F32)
        for i in range(DOF):
            entry = jnp.sum(jrows[i] * vector, axis=1, keepdims=True)
            total = jnp.where(lane24 == i, entry, total)
        return total

    sel_a, sel_s, sel_g, sel_b, sel_r, sel_f = (
        select_ref[first : first + rows].astype(BF16)
        for first, rows in ((0, 24), (24, 8), (32, 8), (40, 32), (72, 8), (80, 24))
    )

    pl.semaphore_wait(barrier, 31)

    def start_phase(phase, rows, sign):
        sbuf[phase] = rows

        def body(step, carry):
            other = lax.rem(sub + step, subs)
            for g in range(GROUPS):
                target = lax.rem(dom + (doms - offsets[g] if sign < 0 else offsets[g]), doms)

                def go():
                    pltpu.make_async_remote_copy(
                        src_ref=sbuf.at[phase, pl.ds(g, 1)],
                        dst_ref=rbuf.at[phase, pl.ds(g * subs + sub, 1)],
                        send_sem=send_sem.at[phase],
                        recv_sem=recv_sem.at[phase],
                        device_id=(target, other),
                        device_id_type=pl.DeviceIdType.MESH,
                    ).start()

                if g == 0:
                    pl.when(step > 0)(go)
                else:
                    go()
            return carry

        lax.fori_loop(0, subs, body, 0)

    def finish_phase(phase):
        whole = rbuf.at[phase, pl.ds(0, 31)]
        pltpu.make_async_copy(whole, whole, recv_sem.at[phase]).wait()
        return rbuf[phase]

    def start_chunk(chunk):
        width = 2560 // CHUNKS

        def body(step, carry):
            other = lax.rem(sub + step, subs)
            for g in range(GROUPS):
                target = lax.rem(dom + doms - offsets[g], doms)

                def go():
                    pltpu.make_async_remote_copy(
                        src_ref=sbig.at[chunk, g],
                        dst_ref=rbig.at[chunk, g * subs + sub],
                        send_sem=bsend_sem.at[chunk],
                        recv_sem=brecv_sem.at[chunk],
                        device_id=(target, other),
                        device_id_type=pl.DeviceIdType.MESH,
                    ).start()

                if g == 0:
                    pl.when(step > 0)(go)
                else:
                    go()
            return carry

        lax.fori_loop(0, subs, body, 0)

    def to_slots(wide):
        lane = lax.broadcasted_iota(jnp.int32, (8, 128), 1)
        pieces = []
        for side in range(4):
            turned = wide if side == 0 else pltpu.roll(wide, 256 - DOF * side, 1)
            pieces.append(jnp.where(lane < DOF, turned[:, 0:128], 0.0))
        return jnp.concatenate(pieces, axis=0)

    def to_elements(slots):
        zero = jnp.zeros((8, 128), F32)
        total = jnp.concatenate([slots[0:8], zero], axis=1)
        for side in range(1, 4):
            wide = jnp.concatenate([slots[8 * side : 8 * side + 8], zero], axis=1)
            total = total + pltpu.roll(wide, DOF * side, 1)
        return total

    def holder_rows(slots):
        stack = jnp.concatenate([slots, pltpu.roll(slots, 64, 1)], axis=0)
        return split_dot(sel_s[:, 0:64], stack)

    def owner_rows(traces):
        stack = jnp.concatenate([traces, pltpu.roll(traces, 64, 1)], axis=0)
        return split_dot(sel_g[:, 0:48], stack)

    def face_sum(slots, arrived):
        stack = jnp.concatenate([slots, arrived, pltpu.roll(arrived, 64, 1)], axis=0)
        total = split_dot(sel_a[:, 0:96], stack)
        return jnp.where(lane24 < DOF, total, 0.0)

    def slot_traces(traces, arrived):
        stack = jnp.concatenate([traces, arrived, pltpu.roll(arrived, 64, 1)], axis=0)
        total = split_dot(sel_b[:, 0:88], stack)
        lane = lax.broadcasted_iota(jnp.int32, (32, 128), 1)
        return jnp.where(lane < DOF, total, 0.0)

    def element_dots(elements, matrix_ref, rows):
        high = elements.astype(BF16).astype(F32)
        both = jnp.concatenate([high, elements - high], axis=0).astype(BF16)[:, 0:200]
        row = lax.broadcasted_iota(jnp.int32, (8, rows), 0)
        total = jnp.zeros((8, rows), F32)
        for e in range(8):
            out = lax.dot_general(both, matrix_ref[e], (((1,), (1,)), ((), ())), preferred_element_type=F32)
            total = jnp.where(row == e, out[0:8] + out[8:16], total)
        return total

    def wide(rows200):
        return jnp.concatenate([rows200, jnp.zeros((8, 56), F32)], axis=1)

    load_slots = to_slots(wide(fload_ref[...]))
    start_phase(0, holder_rows(load_slots), -1)

    blocks = blocks_ref[...]
    picked = jnp.dot(sel_r[:, 0:32], blocks, preferred_element_type=F32)
    width = 2560 // CHUNKS
    for chunk in range(CHUNKS):
        for g in range(GROUPS):
            sbig[chunk, g] = picked[2 * g : 2 * g + 2, chunk * width : (chunk + 1) * width]
    start_chunk(0)
    rhs = face_sum(load_slots, finish_phase(0))
    traces = jacobi(rhs)
    for sweep in range(SWEEPS):
        start_phase(2 * sweep + 1, owner_rows(traces), 1)
        start_chunk(2 * sweep + 1)
        elements = to_elements(slot_traces(traces, finish_phase(2 * sweep + 1)))
        slots = to_slots(wide(element_dots(elements, condensed_ref, 200)))
        start_phase(2 * sweep + 2, holder_rows(slots), -1)
        start_chunk(2 * sweep + 2)
        traces = traces + jacobi(rhs - face_sum(slots, finish_phase(2 * sweep + 2)))
    start_phase(5, owner_rows(traces), 1)
    trace_ref[...] = traces[:, 0:DOF]
    sum_faces = jnp.dot(sel_a[:, 0:32], blocks, preferred_element_type=F32)
    for chunk in range(CHUNKS):
        pltpu.make_async_copy(rbig.at[chunk, pl.ds(0, 31)], rbig.at[chunk, pl.ds(0, 31)], brecv_sem.at[chunk]).wait()
    far = []
    for g in range(GROUPS):
        index = g * subs + partner_ref[g]
        far.append(jnp.concatenate([rbig[chunk, index] for chunk in range(CHUNKS)], axis=1))
    far = jnp.concatenate(far, axis=0).astype(BF16)
    sum_faces = sum_faces + jnp.dot(
        sel_f[:, 0:8], far, preferred_element_type=F32
    )
    faces_ref[...] = sum_faces[:, 0:2500].astype(BF16)
    elements = to_elements(slot_traces(traces, finish_phase(5)))
    state_ref[...] = ((iload_ref[...] - element_dots(elements, imap_ref, 100)) * living_ref[...])
    for phase in range(6):
        whole = rbuf.at[phase, pl.ds(0, 31)]
        pltpu.make_async_copy(whole, whole, send_sem.at[phase]).wait()
    for chunk in range(CHUNKS):
        whole = rbig.at[chunk, pl.ds(0, 31)]
        pltpu.make_async_copy(whole, whole, bsend_sem.at[chunk]).wait()


def one_hots(slot_face, send_slot, recv_face, partner_sub, faces, subs):
    slot_of = slot_face.T.reshape(-1)
    sent = jnp.where(send_slot < 32, send_slot % 4 * 8 + send_slot // 4, -1)
    owned = jnp.where(recv_face < faces, recv_face, -1)
    face = jnp.arange(faces, dtype=jnp.int32)[:, None]
    slot = jnp.arange(32, dtype=jnp.int32)[:, None]
    each_sub = jnp.arange(subs, dtype=jnp.int32)[None, :]

    def from_sub(rows, partners):
        return jnp.where(partners[:, None] == each_sub, rows[:, None], -1).reshape(1, -1)

    def wide(table):
        table = table.astype(F32)
        return jnp.pad(table, ((0, 0), (0, 128 - table.shape[1])))

    holders, owners = partner_sub[:GROUPS], partner_sub[GROUPS:]
    table_a = jnp.concatenate(
        [slot_of[None, :], from_sub(owned[:, 0], holders), from_sub(owned[:, 1], holders)], axis=1
    )
    table_b = jnp.concatenate([from_sub(sent[:, 0], owners), from_sub(sent[:, 1], owners)], axis=1)
    slots_row, faces_row = slot.T, face.T
    pad4 = ((0, 8 - GROUPS), (0, 0))
    table_s = jnp.concatenate([sent[:, 0:1] == slots_row, sent[:, 1:2] == slots_row], axis=1)
    table_g = jnp.concatenate([owned[:, 0:1] == faces_row, owned[:, 1:2] == faces_row], axis=1)
    return jnp.concatenate(
        [
            wide(table_a == face),
            wide(jnp.pad(table_s, pad4)),
            wide(jnp.pad(table_g, pad4)),
            wide(jnp.concatenate([slot_of[:, None] == faces_row, table_b == slot], axis=1)),
            wide(sent.reshape(-1, 1) == slots_row),
            wide(owned.reshape(1, -1) == face),
        ],
        axis=0,
    )


def per_device(
    doms, subs,
    inv_interior, couple_if, couple_fi, face_face, load_interior, load_face, jacobi_inverse,
    slot_face, send_slot, recv_face, partner_sub, elem_count,
):
    elements = load_interior.shape[0]
    interior = load_interior.shape[1]
    face_width = load_face.shape[1]
    face_count = jacobi_inverse.shape[0]
    inverse_blocks = inv_interior.reshape(elements, interior, interior)
    couple_in = couple_if.reshape(elements, interior, face_width)
    couple_out = couple_fi.reshape(elements, face_width, interior)
    face_block = face_face.reshape(elements, face_width, face_width)
    living = (jnp.arange(elements, dtype=jnp.int32) < elem_count[0]).astype(F32)
    interior_map = jnp.einsum(
        "eij,ejk->eik", inverse_blocks, couple_in, preferred_element_type=F32
    ).astype(BF16)
    product = jnp.einsum("eij,ejk->eik", couple_out, interior_map, preferred_element_type=F32)
    condensed = ((face_block.astype(F32) - product) * living[:, None, None]).astype(BF16)
    interior_load = jnp.einsum(
        "eij,ej->ei", inverse_blocks.astype(F32), load_interior, precision=HIGH
    )
    face_load = (
        load_face - jnp.einsum("eij,ej->ei", couple_out.astype(F32), interior_load, precision=HIGH)
    ) * living[:, None]
    shaped = condensed.reshape(elements, 4, DOF, 4, DOF)
    blocks = jnp.concatenate(
        [shaped[:, side, :, side, :].reshape(elements, DOF * DOF) for side in range(4)], axis=0
    )
    blocks = jnp.pad(blocks, ((0, 0), (0, 60)))
    select = one_hots(slot_face, send_slot[0], recv_face[0], partner_sub[0], face_count, subs)
    vmem = pl.BlockSpec(memory_space=pltpu.VMEM)
    return pl.pallas_call(
        functools.partial(exchange_kernel, doms, subs),
        out_shape=(
            jax.ShapeDtypeStruct((face_count, DOF), F32),
            jax.ShapeDtypeStruct((elements, interior), F32),
            jax.ShapeDtypeStruct((face_count, DOF * DOF), BF16),
        ),
        in_specs=[vmem, pl.BlockSpec(memory_space=pltpu.SMEM)] + [vmem] * 7,
        out_specs=(vmem, vmem, vmem),
        scratch_shapes=[
            pltpu.VMEM((24, 2688), F32),
            pltpu.VMEM((DOF, 24, 128), F32),
            pltpu.VMEM((6, 8, 128), F32),
            pltpu.VMEM((6, 32, 128), F32),
            pltpu.VMEM((CHUNKS, GROUPS, 2, 2560 // CHUNKS), F32),
            pltpu.VMEM((CHUNKS, 32, 2, 2560 // CHUNKS), F32),
            pltpu.SemaphoreType.DMA((6,)),
            pltpu.SemaphoreType.DMA((6,)),
            pltpu.SemaphoreType.DMA((CHUNKS,)),
            pltpu.SemaphoreType.DMA((CHUNKS,)),
        ],
        compiler_params=pltpu.CompilerParams(collective_id=0, has_side_effects=True),
    )(select, partner_sub[0], condensed, interior_map, interior_load, face_load, jacobi_inverse, blocks, living[:, None])


def solution(mesh):
    rows = P(("dom", "sub"), None)
    placed = (rows,) * 8 + (P(("dom", "sub"), None, None),) * 2 + (rows, P(("dom", "sub")))
    return jax.shard_map(
        functools.partial(per_device, mesh.shape["dom"], mesh.shape["sub"]),
        mesh=mesh,
        in_specs=placed,
        out_specs=(rows, rows, rows),
        check_vma=False,
    )
```

time: 235 us -> 116 us (0.49); the launches traced: 231 us -> 115 us
  starting transfers between devices: 91.2 us -> 0 us
  Pallas kernels: 0 us -> 56.6 us
  waiting for transfers between devices: 46.9 us -> 0 us
  blocking collectives: 26.9 us -> 0 us
  matrix products: 7.21 us -> 2.72 us
    ppermute x18 -> x0, starting transfers between devices: 73.7 us -> none  [from_behind(): lax.ppermute(array, axis, [(i, (i + by) % length) for i in range(length)])]
    pallas_call x0 -> x1, Pallas kernels: none -> 56.6 us  [per_device(): pl.pallas_call(functools.partial(exchange_kernel, doms, subs), out_shape=...]
    all_to_all x3 -> x0, waiting for transfers between devices: 32.4 us -> none  [summed_on_arrival(): lax.all_to_all(tiles, axis, split_axis=0, concat_axis=0, tiled=True)]
    all_to_all x3 -> x0, blocking collectives: 26.9 us -> none  [summed_on_arrival(): lax.all_to_all(tiles, axis, split_axis=0, concat_axis=0, tiled=True)]
    all_to_all x3 -> x0, starting transfers between devices: 17.5 us -> none  [summed_on_arrival(): lax.all_to_all(tiles, axis, split_axis=0, concat_axis=0, tiled=True)]
    ppermute x18 -> x0, waiting for transfers between devices: 14.5 us -> none  [from_behind(): lax.ppermute(array, axis, [(i, (i + by) % length) for i in range(length)])]
    dot_general x20 -> x2, matrix products: 6.37 us -> 1.17 us  [the longest x1 0.75 us: per_device(): jnp.einsum('eij,ej->ei', couple_out.astype(F32), interior_load, precision...]
    gather x7 -> x0, local copies, waits for them, and re-layouts: 3.45 us -> none  [pick_rows(): return padded[index_table]]
  transfers between devices with their start and end apart: 21 -> 0, of which waited for: 12 -> 0; matrix products, arithmetic and copies ran while one was open for 1% -> 0% of each run, Pallas kernels for 0% -> 0%
where the time goes in v1:
time: 116 us; the launch traced here: 115 us
  Pallas kernels  56.6 us (49%)
  other arithmetic  34.1 us (29%)
  local copies, waits for them, and re-layouts  20 us (17%)
  matrix products  2.72 us (2%)
  between operations  1.46 us (1%)
    pallas_call x1, Pallas kernels, per_device(): pl.pallas_call(functools.partial(exchange_kernel, doms, subs), out_shape=...  56.6 us
    unnamed x3, other arithmetic  16.4 us
    convert_element_type x1, other arithmetic, per_device(): face_block.astype(F32) - product  13 us
    unnamed x20, local copies, waits for them, and re-layouts  5.77 us
    slice x1, local copies, waits for them, and re-layouts, per_device(): shaped[:, side, :, side, :].reshape(elements, DOF * DOF)  2.56 us
    convert_element_type x1, local copies, waits for them, and re-layouts, per_device(): face_block.astype(F32) - product  2.37 us

profile of v1, /device:TPU:1, one launch (start us, length us, event | category | flops | bytes accessed | tf_op | source)
XLA Modules:
  0.0 114.9 jit_solution(7175558906695932)
XLA Ops:
  0.6 0.7 compare_select_fusion.3
  1.4 0.8 slice_bitcast_fusion
  2.2 0.7 compare_select_fusion
  2.9 0.1 select_n.100
  3.0 0.1 select_n.98
  3.1 0.8 broadcast_in_dim_reshape.4
  3.9 0.1 add_bitcast_fusion
  4.0 0.1 pad_add_fusion.1
  4.2 0.1 pad_add_fusion.2
  4.3 0.1 select_n.107
  4.4 0.1 select_n.105
  4.5 0.1 add_bitcast_fusion.1
  4.6 0.8 eq.219
  5.3 0.1 iota_compare_fusion.2
  5.4 0.1 pad_add_fusion
  5.5 0.8 copy.35
  6.3 0.1 squeeze.19
  6.4 0.1 iota_compare_fusion.6
  6.5 0.8 copy.36
  7.2 0.1 squeeze.20
  7.3 0.6 concatenate.29.select_ref
  8.0 13.0 %convert_reduce_fusion = f32[320000]{0:T(1024)S(1)} fusion(bf16[1,320000]{1,0:T(2,128)(2,1)} %param.15), kind=kLoop, calls=%fused_computation.3 | loop fusion | flops 320000 | bytes 1920000 | tf_op jit(solution)/shard_map/convert_element_type | solution.py:288
  20.9 2.4 %reshape.242 = f32[8,200,200]{2,1,0:T(8,128)S(1)} reshape(f32[320000]{0:T(1024)S(1)} %convert_reduce_fusion) | data formatting | bytes 2560000 | tf_op jit(solution)/shard_map/convert_element_type | solution.py:288
  23.3 7.6 %reduce.3 = bf16[160000]{0:T(1024)(128)(2,1)S(1)} reduce(bf16[1,160000]{1,0:T(2,128)(2,1)} %param.14, bf16[]{:T(256)} %constant.79), dimensions={0}, to_apply=%param.14.reduce_sub_computation | reduce | bytes 640002 | tf_op args[2]
  31.0 1.6 %reshape.240 = bf16[8,200,100]{2,1,0:T(8,128)(2,1)S(1)} reshape(bf16[160000]{0:T(1024)(128)(2,1)S(1)} %reduce.3) | data formatting | bytes 640000 | tf_op jit(solution)/shard_map/reshape | solution.py:281
  33.2 0.9 reduce.1
  34.2 0.3 reshape.238
  34.5 7.8 %reduce.2 = bf16[160000]{0:T(1024)(128)(2,1)S(1)} reduce(bf16[1,160000]{1,0:T(2,128)(2,1)} %param.13, bf16[]{:T(256)} %constant.79), dimensions={0}, to_apply=%param.13.reduce_sub_computation | reduce | bytes 640002 | tf_op args[1]
  42.3 0.8 reshape.239
  43.1 1.2 %fusion.22 = bf16[8,100,200]{1,2,0:T(8,128)(2,1)} fusion(bf16[8,100,100]{2,1,0:T(8,128)(2,1)S(1)} %reshape.238, bf16[8,100,200]{2,1,0:T(8,128)(2,1)S(1)} %reshape.239), kind=kOutput, calls=%fused_computation.75 | convolution fusion | flops 32000000 | bytes 800000 | tf_op jit(solution)/shard_map/eij,ejk->eik/dot_general | solution.py:284
  44.3 1.4 %copy.38 = bf16[8,100,200]{2,0,1:T(8,128)(2,1)S(1)} copy(bf16[8,100,200]{1,2,0:T(8,128)(2,1)} %fusion.22) | data formatting | bytes 640000 | tf_op jit(solution)/shard_map/eij,ejk->eik/dot_general | solution.py:284
  45.6 0.4 fusion.1.condensed_ref
  46.0 0.9 copy.45.imap_ref
  46.9 0.4 fusion.23
  47.4 0.7 fusion.10
  48.1 0.7 fusion.9.fload_ref
  48.8 0.8 reshape.241
  49.7 2.6 %slice_reduce_fusion.3 = (bf16[8,50,50]{2,1,0:T(8,128)(2,1)S(1)}, bf16[8,50,50]{2,1,0:T(8,128)(2,1)S(1)}, bf16[8,50,50]{2,1,0:T(8,128)(2,1)S(1)}, bf16[8,50,50]{2,1,0:T(8,128)(2,1)S(1)}) fusion(bf16[8,4,50,4,50]{4,3,2,1,0:T(4,128)(2,1)S(1)} %reshape.241), kind=kLoop, calls=%fused_computation.12 | loop fusion | bytes 320000 | tf_op jit(solution)/shard_map/slice | solution.py:297
  52.2 0.1 reshape_squeeze.15
  52.4 0.2 reshape_squeeze.14
  52.5 0.2 reshape_squeeze.13
  52.7 0.2 reshape_squeeze.12
  52.9 0.7 fusion.8.blocks_ref
  53.5 0.6 fusion.12.living_ref
  54.1 56.6 %shard_map.139 = (f32[24,50]{1,0:T(8,128)}, f32[8,100]{1,0:T(8,128)}, bf16[24,2500]{1,0:T(8,128)(2,1)}) custom-call(f32[104,128]{1,0:T(8,128)} %concatenate.29.select_ref, s32[8]{0:T(128)} %bitcast.61, bf16[8,200,200]{2,1,0:T(8,128)(2,1)} %copy-done.1, bf16[8,100,200]{2,1,0:T(8,128)(2,1)} %copy.45.imap_ref, f32[8,100]{1,0:T(8,128)} %bitcast.58, ...), custom_call_target="tpu_custom_call" | custom-call | tf_op jit(solution)/shard_map/pallas_call | solution.py:302
  110.8 1.3 %copy.68 = f32[24,50]{1,0:T(8,128)} copy(f32[24,50]{1,0:T(8,128)} %get-tuple-element.26) | data formatting | bytes 9600
  112.1 1.3 %copy.69 = f32[8,100]{1,0:T(8,128)} copy(f32[8,100]{1,0:T(8,128)} %get-tuple-element.27) | data formatting | bytes 6400
  113.3 1.6 %copy.70 = bf16[24,2500]{1,0:T(8,128)(2,1)} copy(bf16[24,2500]{1,0:T(8,128)(2,1)} %get-tuple-element.28) | data formatting | bytes 240000
  (27 shorter events, 0.4 us)
Async XLA Ops:
  0.6 46.3 %copy-start = (f32[8,100]{1,0:T(8,128)S(1)}, f32[8,100]{1,0:T(8,128)}, u32[]{:S(2)}) copy-start(f32[8,100]{1,0:T(8,128)} %param.16) | copy-start | bytes 9604
  23.3 9.9 %copy-start.2 = (bf16[1,80000]{1,0:T(2,128)(2,1)S(1)}, bf16[1,80000]{1,0:T(2,128)(2,1)}, u32[]{:S(2)}) copy-start(bf16[1,80000]{1,0:T(2,128)(2,1)} %param.12) | copy-start | bytes 480004
  45.6 2.5 %copy-start.4 = (f32[8,200]{1,0:T(8,128)S(1)}, f32[8,200]{1,0:T(8,128)}, u32[]{:S(2)}) copy-start(f32[8,200]{1,0:T(8,128)} %param.17) | copy-start | bytes 19204
  46.0 3.6 %copy-start.1 = (bf16[8,200,200]{2,1,0:T(8,128)(2,1)}, bf16[8,200,200]{2,1,0:T(8,128)(2,1)S(1)}, u32[]{:S(2)}) copy-start(bf16[8,200,200]{2,1,0:T(8,128)(2,1)S(1)} %fusion.1.condensed_ref) | copy-start | bytes 1920004
  47.4 4.9 %copy-start.3 = (f32[8,1,100]{2,1,0:T(1,128)}, f32[8,1,100]{2,1,0:T(1,128)S(1)}, u32[]{:S(2)}) copy-start(f32[8,1,100]{2,1,0:T(1,128)S(1)} %fusion.23) | copy-start | bytes 9604

commit v2 on v1

--- a/solution.py
+++ b/solution.py
@@ -29,7 +29,8 @@
 
 def exchange_kernel(
     doms, subs,
-    select_ref, partner_ref, condensed_ref, imap_ref, iload_ref, fload_ref, jac_ref, blocks_ref, living_ref,
+    slot_ref, send_ref, recv_ref, partner_ref,
+    condensed_ref, imap_ref, iload_ref, fload_ref, jac_ref, blocks_ref, living_ref,
     trace_ref, state_ref, faces_ref,
     jflat, jrows, sbuf, rbuf, sbig, rbig, send_sem, recv_sem, bsend_sem, brecv_sem,
 ):
@@ -74,10 +75,7 @@
             total = jnp.where(lane24 == i, entry, total)
         return total
 
-    sel_a, sel_s, sel_g, sel_b, sel_r, sel_f = (
-        select_ref[first : first + rows].astype(BF16)
-        for first, rows in ((0, 24), (24, 8), (32, 8), (40, 32), (72, 8), (80, 24))
-    )
+    sel_a, sel_s, sel_g, sel_b, sel_r, sel_f = one_hots(slot_ref, send_ref, recv_ref, partner_ref, subs)
 
     pl.semaphore_wait(barrier, 31)
 
@@ -213,7 +211,7 @@
         pltpu.make_async_copy(rbig.at[chunk, pl.ds(0, 31)], rbig.at[chunk, pl.ds(0, 31)], brecv_sem.at[chunk]).wait()
     far = []
     for g in range(GROUPS):
-        index = g * subs + partner_ref[g]
+        index = g * subs + partner_ref[0, g]
         far.append(jnp.concatenate([rbig[chunk, index] for chunk in range(CHUNKS)], axis=1))
     far = jnp.concatenate(far, axis=0).astype(BF16)
     sum_faces = sum_faces + jnp.dot(
@@ -230,41 +228,61 @@
         pltpu.make_async_copy(whole, whole, bsend_sem.at[chunk]).wait()
 
 
-def one_hots(slot_face, send_slot, recv_face, partner_sub, faces, subs):
-    slot_of = slot_face.T.reshape(-1)
-    sent = jnp.where(send_slot < 32, send_slot % 4 * 8 + send_slot // 4, -1)
-    owned = jnp.where(recv_face < faces, recv_face, -1)
-    face = jnp.arange(faces, dtype=jnp.int32)[:, None]
-    slot = jnp.arange(32, dtype=jnp.int32)[:, None]
-    each_sub = jnp.arange(subs, dtype=jnp.int32)[None, :]
-
-    def from_sub(rows, partners):
-        return jnp.where(partners[:, None] == each_sub, rows[:, None], -1).reshape(1, -1)
-
-    def wide(table):
-        table = table.astype(F32)
-        return jnp.pad(table, ((0, 0), (0, 128 - table.shape[1])))
-
-    holders, owners = partner_sub[:GROUPS], partner_sub[GROUPS:]
-    table_a = jnp.concatenate(
-        [slot_of[None, :], from_sub(owned[:, 0], holders), from_sub(owned[:, 1], holders)], axis=1
-    )
-    table_b = jnp.concatenate([from_sub(sent[:, 0], owners), from_sub(sent[:, 1], owners)], axis=1)
-    slots_row, faces_row = slot.T, face.T
-    pad4 = ((0, 8 - GROUPS), (0, 0))
-    table_s = jnp.concatenate([sent[:, 0:1] == slots_row, sent[:, 1:2] == slots_row], axis=1)
-    table_g = jnp.concatenate([owned[:, 0:1] == faces_row, owned[:, 1:2] == faces_row], axis=1)
-    return jnp.concatenate(
-        [
-            wide(table_a == face),
-            wide(jnp.pad(table_s, pad4)),
-            wide(jnp.pad(table_g, pad4)),
-            wide(jnp.concatenate([slot_of[:, None] == faces_row, table_b == slot], axis=1)),
-            wide(sent.reshape(-1, 1) == slots_row),
-            wide(owned.reshape(1, -1) == face),
-        ],
-        axis=0,
-    )
+def one_hots(slot_ref, send_ref, recv_ref, partner_ref, subs):
+    lane = lax.broadcasted_iota(jnp.int32, (8, 128), 1)
+    row = lax.broadcasted_iota(jnp.int32, (8, 128), 0)
+    row24 = lax.broadcasted_iota(jnp.int32, (24, 128), 0)
+    row32 = lax.broadcasted_iota(jnp.int32, (32, 128), 0)
+    nothing = jnp.full((8, 128), -1, jnp.int32)
+    no = jnp.zeros((8, 128), F32)
+    table_a, table_b, table_f, hot_s, hot_g, hot_r, local_b = nothing, nothing, nothing, no, no, no, []
+    for side in range(4):
+        column = nothing
+        for e in range(8):
+            face = slot_ref[side, e]
+            face = jnp.where(face < 24, face, -1)
+            table_a = jnp.where(lane == 8 * side + e, face, table_a)
+            column = jnp.where(row == e, face, column)
+        local_b.append((lane == column).astype(F32))
+    for g in range(GROUPS):
+        holder, owner = partner_ref[0, g], partner_ref[0, GROUPS + g]
+        for r in range(2):
+            face, slot = recv_ref[0, r, g], send_ref[0, r, g]
+            face = jnp.where(face < 24, face, -1000)
+            slot = jnp.where(slot < 32, (slot & 3) * 8 + (slot >> 2), -1000)
+            table_a = jnp.where(lane == 32 + 32 * r + subs * g + holder, face, table_a)
+            table_b = jnp.where(lane == 24 + 32 * r + subs * g + owner, slot, table_b)
+            table_f = jnp.where(lane == 2 * g + r, face, table_f)
+            hot_s = jnp.where((row == g) & (lane == 32 * r + slot), 1.0, hot_s)
+            hot_g = jnp.where((row == g) & (lane == 24 * r + face), 1.0, hot_g)
+            hot_r = jnp.where((row == 2 * g + r) & (lane == slot), 1.0, hot_r)
+
+    def equal(rows, table):
+        return (rows == jnp.concatenate([table] * (rows.shape[0] // 8), axis=0)).astype(F32)
+
+    hot_b = equal(row32, table_b) + jnp.concatenate(local_b, axis=0)
+    hots = (equal(row24, table_a), hot_s, hot_g, hot_b, hot_r, equal(row24, table_f))
+    return tuple(hot.astype(BF16) for hot in hots)
+
+
+def squeeze_kernel(*refs):
+    half = len(refs) // 2
+    for source, target in zip(refs[:half], refs[half:]):
+        rows = target.shape[0]
+        for first in range(0, rows, 16):
+            count = min(16, rows - first)
+            line = source[0:1, 128 * first : 128 * (first + count)].astype(F32)
+            target[first : first + count, :] = line.reshape(count, 128).astype(BF16)
+
+
+def squeezed(*arrays):
+    vmem = pl.BlockSpec(memory_space=pltpu.VMEM)
+    return pl.pallas_call(
+        squeeze_kernel,
+        out_shape=[jax.ShapeDtypeStruct((array.shape[1] // 128, 128), BF16) for array in arrays],
+        in_specs=[vmem] * len(arrays),
+        out_specs=[vmem] * len(arrays),
+    )(*arrays)
 
 
 def per_device(
@@ -276,6 +294,7 @@
     interior = load_interior.shape[1]
     face_width = load_face.shape[1]
     face_count = jacobi_inverse.shape[0]
+    inv_interior, couple_if, couple_fi, face_face = squeezed(inv_interior, couple_if, couple_fi, face_face)
     inverse_blocks = inv_interior.reshape(elements, interior, interior)
     couple_in = couple_if.reshape(elements, interior, face_width)
     couple_out = couple_fi.reshape(elements, face_width, interior)
@@ -297,7 +316,6 @@
         [shaped[:, side, :, side, :].reshape(elements, DOF * DOF) for side in range(4)], axis=0
     )
     blocks = jnp.pad(blocks, ((0, 0), (0, 60)))
-    select = one_hots(slot_face, send_slot[0], recv_face[0], partner_sub[0], face_count, subs)
     vmem = pl.BlockSpec(memory_space=pltpu.VMEM)
     return pl.pallas_call(
         functools.partial(exchange_kernel, doms, subs),
@@ -306,7 +324,7 @@
             jax.ShapeDtypeStruct((elements, interior), F32),
             jax.ShapeDtypeStruct((face_count, DOF * DOF), BF16),
         ),
-        in_specs=[vmem, pl.BlockSpec(memory_space=pltpu.SMEM)] + [vmem] * 7,
+        in_specs=[pl.BlockSpec(memory_space=pltpu.SMEM)] * 4 + [vmem] * 7,
         out_specs=(vmem, vmem, vmem),
         scratch_shapes=[
             pltpu.VMEM((24, 2688), F32),
@@ -321,7 +339,7 @@
             pltpu.SemaphoreType.DMA((CHUNKS,)),
         ],
         compiler_params=pltpu.CompilerParams(collective_id=0, has_side_effects=True),
-    )(select, partner_sub[0], condensed, interior_map, interior_load, face_load, jacobi_inverse, blocks, living[:, None])
+    )(slot_face.T, send_slot.transpose(0, 2, 1), recv_face.transpose(0, 2, 1), partner_sub, condensed, interior_map, interior_load, face_load, jacobi_inverse, blocks, living[:, None])
 
 
 def solution(mesh):

time: 116 us -> 83.9 us (0.72)
  other arithmetic: 34.1 us -> 1.96 us
  local copies, waits for them, and re-layouts: 20 us -> 16.7 us
  Pallas kernels: 56.6 us -> 59.8 us
    unnamed x3 -> x0, other arithmetic: 16.4 us -> none
    convert_element_type x1 -> x0, other arithmetic: 13 us -> none  [per_device(): face_block.astype(F32) - product]
    pallas_call x0 -> x1, Pallas kernels: none -> 3.14 us  [squeezed(): pl.pallas_call(squeeze_kernel, out_shape=[jax.ShapeDtypeStruct((array.sha...]
    unnamed x20 -> x17, local copies, waits for them, and re-layouts: 5.77 us -> 4.17 us
    eq x3 -> x0, local copies, waits for them, and re-layouts: 1.58 us -> none  [the longest x1 0.8 us: from_sub(): partners[:, None] == each_sub]
    select_n x5 -> x0, other arithmetic: 1.47 us -> none  [the longest x2 0.71 us: one_hots(): sent = jnp.where(send_slot < 32, send_slot % 4 * 8 + send_slot // 4, -1)]
    convert_element_type x1, local copies, waits for them, and re-layouts: 2.37 us -> 3.59 us  [per_device(): face_block.astype(F32) - product]
where the time goes in v2:
time: 83.9 us; the launch traced here: 82.6 us
  Pallas kernels  59.8 us (71%)
  local copies, waits for them, and re-layouts  16.7 us (20%)
  matrix products  2.73 us (3%)
  other arithmetic  1.96 us (2%)
  between operations  1.44 us (2%)
    pallas_call x1, Pallas kernels, per_device(): pl.pallas_call(functools.partial(exchange_kernel, doms, subs), out_shape=...  56.6 us
    unnamed x17, local copies, waits for them, and re-layouts  4.17 us
    convert_element_type x1, local copies, waits for them, and re-layouts, per_device(): face_block.astype(F32) - product  3.59 us
    pallas_call x1, Pallas kernels, squeezed(): pl.pallas_call(squeeze_kernel, out_shape=[jax.ShapeDtypeStruct((array.sha...  3.14 us
    slice x1, local copies, waits for them, and re-layouts, per_device(): shaped[:, side, :, side, :].reshape(elements, DOF * DOF)  2.56 us

profile of v2, /device:TPU:1, one launch (start us, length us, event | category | flops | bytes accessed | tf_op | source)
XLA Modules:
  0.0 82.6 jit_solution(90160055737608215)
XLA Ops:
  0.6 0.0 copy-start
  0.6 3.1 %shard_map.139 = (bf16[625,128]{1,0:T(8,128)(2,1)}, bf16[1250,128]{1,0:T(8,128)(2,1)}, bf16[1250,128]{1,0:T(8,128)(2,1)}, bf16[2500,128]{1,0:T(8,128)(2,1)}) custom-call(bf16[1,80000]{1,0:T(2,128)(2,1)} %refs_0_.1, bf16[1,160000]{1,0:T(2,128)(2,1)} %refs_1_.1, bf16[1,160000]{1,0:T(2,128)(2,1)} %refs_2_.1, bf16[1,320000]{1,0:T(2,128)(2,1)} %refs_3_.1), custom_call_target="tpu_custom_call" | custom-call | tf_op jit(solution)/shard_map/pallas_call | solution.py:280
  3.8 0.0 copy-start.3
  3.8 0.0 copy-start.4
  3.8 0.0 copy-start.2
  3.8 3.6 %reshape.41 = f32[8,200,200]{2,1,0:T(8,128)S(1)} reshape(bf16[2500,128]{1,0:T(8,128)(2,1)} %get-tuple-element.7) | data formatting | bytes 1920000 | tf_op jit(solution)/shard_map/convert_element_type | solution.py:307
  7.4 0.0 copy-done.3
  7.4 1.6 %reshape.37 = bf16[8,200,100]{2,1,0:T(8,128)(2,1)S(1)} reshape(bf16[1250,128]{1,0:T(8,128)(2,1)S(1)} %copy-done.3) | data formatting | bytes 640000 | tf_op jit(solution)/shard_map/reshape | solution.py:300
  9.6 0.0 copy-done.4
  9.7 0.3 reshape.38
  10.0 0.0 copy-done.2
  10.0 0.8 reshape.39
  10.8 1.2 %fusion.12 = bf16[8,100,200]{1,2,0:T(8,128)(2,1)} fusion(bf16[8,100,100]{2,1,0:T(8,128)(2,1)S(1)} %reshape.38, bf16[8,100,200]{2,1,0:T(8,128)(2,1)S(1)} %reshape.39), kind=kOutput, calls=%fused_computation.21 | convolution fusion | flops 32000000 | bytes 800000 | tf_op jit(solution)/shard_map/eij,ejk->eik/dot_general | solution.py:303
  12.0 1.4 %copy.30 = bf16[8,100,200]{2,0,1:T(8,128)(2,1)S(1)} copy(bf16[8,100,200]{1,2,0:T(8,128)(2,1)} %fusion.12) | data formatting | bytes 640000 | tf_op jit(solution)/shard_map/eij,ejk->eik/dot_general | solution.py:303
  13.3 0.0 copy-start.6
  13.3 0.4 multiply_convert_fusion.condensed_ref
  13.7 0.0 copy-start.1
  13.7 0.9 %copy.36.imap_ref = bf16[8,100,200]{2,1,0:T(8,128)(2,1)} copy(bf16[8,100,200]{2,0,1:T(8,128)(2,1)S(1)} %copy.30) | data formatting | bytes 640000 | tf_op jit(solution)/shard_map/convert_element_type | solution.py:305
  14.6 0.0 copy-done
  14.6 0.4 fusion.13
  15.1 0.0 copy-start.5
  15.1 0.7 fusion.8
  15.8 0.0 copy-done.6
  15.8 0.7 fusion.7.fload_ref
  16.5 0.8 %reshape.40 = bf16[8,4,50,4,50]{4,3,2,1,0:T(4,128)(2,1)S(1)} reshape(bf16[8,200,200]{2,1,0:T(8,128)(2,1)S(1)} %multiply_convert_fusion.condensed_ref) | data formatting | bytes 1280000 | tf_op jit(solution)/shard_map/reshape | solution.py:314
  17.4 0.0 copy-done.1
  17.4 2.6 %slice_reduce_fusion.3 = (bf16[8,50,50]{2,1,0:T(8,128)(2,1)S(1)}, bf16[8,50,50]{2,1,0:T(8,128)(2,1)S(1)}, bf16[8,50,50]{2,1,0:T(8,128)(2,1)S(1)}, bf16[8,50,50]{2,1,0:T(8,128)(2,1)S(1)}) fusion(bf16[8,4,50,4,50]{4,3,2,1,0:T(4,128)(2,1)S(1)} %reshape.40), kind=kLoop, calls=%fused_computation.9 | loop fusion | bytes 320000 | tf_op jit(solution)/shard_map/slice | solution.py:316
  20.0 0.0 copy-done.5
  20.0 0.1 reshape_squeeze.15
  20.1 0.2 reshape_squeeze.14
  20.3 0.2 reshape_squeeze.13
  20.4 0.2 reshape_squeeze.12
  20.6 0.7 fusion.6.blocks_ref
  21.2 0.6 fusion.10.living_ref
  21.8 56.6 %shard_map.140 = (f32[24,50]{1,0:T(8,128)}, f32[8,100]{1,0:T(8,128)}, bf16[24,2500]{1,0:T(8,128)(2,1)}) custom-call(s32[4,8]{1,0:T(4,128)} %bitcast.28, s32[1,2,4]{2,1,0:T(2,128)} %bitcast.29, s32[1,2,4]{2,1,0:T(2,128)} %bitcast.30, s32[1,8]{1,0:T(1,128)} %partner_ref.1, bf16[8,200,200]{2,1,0:T(8,128)(2,1)} %copy-done.1, ...), custom_call_target="tpu_custom_call" | custom-call | tf_op jit(solution)/shard_map/pallas_call | solution.py:320
  78.5 1.3 %copy.53 = f32[24,50]{1,0:T(8,128)} copy(f32[24,50]{1,0:T(8,128)} %get-tuple-element.18) | data formatting | bytes 9600
  79.8 1.3 %copy.54 = f32[8,100]{1,0:T(8,128)} copy(f32[8,100]{1,0:T(8,128)} %get-tuple-element.19) | data formatting | bytes 6400
  81.1 1.6 %copy.55 = bf16[24,2500]{1,0:T(8,128)(2,1)} copy(bf16[24,2500]{1,0:T(8,128)(2,1)} %get-tuple-element.20) | data formatting | bytes 240000
  (1 shorter events, 0.0 us)
Async XLA Ops:
  0.6 14.0 %copy-start = (f32[8,100]{1,0:T(8,128)S(1)}, f32[8,100]{1,0:T(8,128)}, u32[]{:S(2)}) copy-start(f32[8,100]{1,0:T(8,128)} %param.16) | copy-start | bytes 9604
  3.8 3.6 %copy-start.3 = (bf16[1250,128]{1,0:T(8,128)(2,1)S(1)}, bf16[1250,128]{1,0:T(8,128)(2,1)}, u32[]{:S(2)}) copy-start(bf16[1250,128]{1,0:T(8,128)(2,1)} %get-tuple-element.8) | copy-start | bytes 960004
  3.8 5.9 %copy-start.4 = (bf16[625,128]{1,0:T(8,128)(2,1)S(1)}, bf16[625,128]{1,0:T(8,128)(2,1)}, u32[]{:S(2)}) copy-start(bf16[625,128]{1,0:T(8,128)(2,1)} %get-tuple-element.9) | copy-start | bytes 480004
  3.8 6.2 %copy-start.2 = (bf16[1250,128]{1,0:T(8,128)(2,1)S(1)}, bf16[1250,128]{1,0:T(8,128)(2,1)}, u32[]{:S(2)}) copy-start(bf16[1250,128]{1,0:T(8,128)(2,1)} %get-tuple-element.10) | copy-start | bytes 960004
  13.3 2.5 %copy-start.6 = (f32[8,200]{1,0:T(8,128)S(1)}, f32[8,200]{1,0:T(8,128)}, u32[]{:S(2)}) copy-start(f32[8,200]{1,0:T(8,128)} %param.17) | copy-start | bytes 19204
  13.7 3.6 %copy-start.1 = (bf16[8,200,200]{2,1,0:T(8,128)(2,1)}, bf16[8,200,200]{2,1,0:T(8,128)(2,1)S(1)}, u32[]{:S(2)}) copy-start(bf16[8,200,200]{2,1,0:T(8,128)(2,1)S(1)} %multiply_convert_fusion.condensed_ref) | copy-start | bytes 1920004
  15.1 4.9 %copy-start.5 = (f32[8,1,100]{2,1,0:T(1,128)}, f32[8,1,100]{2,1,0:T(1,128)S(1)}, u32[]{:S(2)}) copy-start(f32[8,1,100]{2,1,0:T(1,128)S(1)} %fusion.13) | copy-start | bytes 9604

commit v3 on v2

--- a/solution.py
+++ b/solution.py
@@ -29,12 +29,22 @@
 
 def exchange_kernel(
     doms, subs,
-    slot_ref, send_ref, recv_ref, partner_ref,
-    condensed_ref, imap_ref, iload_ref, fload_ref, jac_ref, blocks_ref, living_ref,
+    slot_ref, send_ref, recv_ref, partner_ref, count_ref,
+    inv_hbm, cif_hbm, cfi_hbm, ff_hbm, load_ref, fload_ref, jac_ref,
     trace_ref, state_ref, faces_ref,
     jflat, jrows, sbuf, rbuf, sbig, rbig, send_sem, recv_sem, bsend_sem, brecv_sem,
+    inv_ref, cif_ref, cfi_ref, ff_ref, in_sem, condensed_ref, imap_ref, iload_ref, face_load_ref, blocks_ref,
+    *spaces,
 ):
     dom, sub = lax.axis_index("dom"), lax.axis_index("sub")
+    loads = [
+        pltpu.make_async_copy(source, target, in_sem.at[k])
+        for k, (source, target) in enumerate(
+            ((inv_hbm, inv_ref), (cfi_hbm, cfi_ref), (cif_hbm, cif_ref), (ff_hbm, ff_ref))
+        )
+    ]
+    for load in loads:
+        load.start()
     offsets = [group_offset(g, doms) for g in range(GROUPS)]
     for phase in range(6):
         rbuf[phase] = jnp.zeros(rbuf.shape[1:], F32)
@@ -55,6 +65,11 @@
         return carry
 
     lax.fori_loop(0, subs, greet, 0)
+
+    condense_body(
+        loads, inv_ref, cif_ref, cfi_ref, ff_ref, load_ref, fload_ref, count_ref,
+        condensed_ref, imap_ref, iload_ref, face_load_ref, blocks_ref, *spaces,
+    )
 
     jflat[:, 0:2500] = jac_ref[...].astype(F32)
     jflat[:, 2500:2688] = jnp.zeros((24, 188), F32)
@@ -66,7 +81,6 @@
         jrows[i] = pltpu.roll(window, 256 - (start - base), 1)[:, 0:128]
 
     lane24 = lax.broadcasted_iota(jnp.int32, (24, 128), 1)
-    row8 = lax.broadcasted_iota(jnp.int32, (8, 200), 0)
 
     def jacobi(vector):
         total = jnp.zeros((24, 128), F32)
@@ -184,7 +198,7 @@
     def wide(rows200):
         return jnp.concatenate([rows200, jnp.zeros((8, 56), F32)], axis=1)
 
-    load_slots = to_slots(wide(fload_ref[...]))
+    load_slots = to_slots(wide(face_load_ref[...]))
     start_phase(0, holder_rows(load_slots), -1)
 
     blocks = blocks_ref[...]
@@ -205,7 +219,7 @@
         start_chunk(2 * sweep + 2)
         traces = traces + jacobi(rhs - face_sum(slots, finish_phase(2 * sweep + 2)))
     start_phase(5, owner_rows(traces), 1)
-    trace_ref[...] = traces[:, 0:DOF]
+    trace_ref[...] = traces
     sum_faces = jnp.dot(sel_a[:, 0:32], blocks, preferred_element_type=F32)
     for chunk in range(CHUNKS):
         pltpu.make_async_copy(rbig.at[chunk, pl.ds(0, 31)], rbig.at[chunk, pl.ds(0, 31)], brecv_sem.at[chunk]).wait()
@@ -217,9 +231,12 @@
     sum_faces = sum_faces + jnp.dot(
         sel_f[:, 0:8], far, preferred_element_type=F32
     )
-    faces_ref[...] = sum_faces[:, 0:2500].astype(BF16)
+    faces_ref[...] = sum_faces
     elements = to_elements(slot_traces(traces, finish_phase(5)))
-    state_ref[...] = ((iload_ref[...] - element_dots(elements, imap_ref, 100)) * living_ref[...])
+    row100 = lax.broadcasted_iota(jnp.int32, (8, 100), 0)
+    state = iload_ref[...] - element_dots(elements, imap_ref, 100)
+    state = jnp.where(row100 < count_ref[0], state, 0.0)
+    state_ref[...] = jnp.concatenate([state, jnp.zeros((8, 28), F32)], axis=1)
     for phase in range(6):
         whole = rbuf.at[phase, pl.ds(0, 31)]
         pltpu.make_async_copy(whole, whole, send_sem.at[phase]).wait()
@@ -265,24 +282,124 @@
     return tuple(hot.astype(BF16) for hot in hots)
 
 
-def squeeze_kernel(*refs):
-    half = len(refs) // 2
-    for source, target in zip(refs[:half], refs[half:]):
-        rows = target.shape[0]
-        for first in range(0, rows, 16):
-            count = min(16, rows - first)
-            line = source[0:1, 128 * first : 128 * (first + count)].astype(F32)
-            target[first : first + count, :] = line.reshape(count, 128).astype(BF16)
-
-
-def squeezed(*arrays):
-    vmem = pl.BlockSpec(memory_space=pltpu.VMEM)
-    return pl.pallas_call(
-        squeeze_kernel,
-        out_shape=[jax.ShapeDtypeStruct((array.shape[1] // 128, 128), BF16) for array in arrays],
-        in_specs=[vmem] * len(arrays),
-        out_specs=[vmem] * len(arrays),
-    )(*arrays)
+def squeeze(source, flat):
+    rows = source.shape[1] // 128
+    for first in range(0, rows, 16):
+        count = min(16, rows - first)
+        line = source[0:1, 128 * first : 128 * (first + count)].astype(F32)
+        flat[first : first + count, :] = line.reshape(count, 128)
+
+
+def spread_rows(flat, mid, width, count, pitch):
+    lane = lax.broadcasted_iota(jnp.int32, (count, 128), 1)
+    for i in range(3200 // width):
+        first, off = divmod(width * i, 128)
+        last = (off + width - 1) // 128
+        turned = []
+        for tile in range(last + 1):
+            value = flat[pl.ds(first + tile, count, stride=25), :]
+            turned.append(pltpu.roll(value, 128 - off, 1) if off else value)
+        for tile in range((width + 127) // 128):
+            value = turned[tile]
+            if off and tile < last:
+                value = jnp.where(lane < 128 - off, value, turned[tile + 1])
+            mid[tile, pl.ds(i * pitch, count), :] = value
+
+
+def matrix_rows(mid, tile, first, rows, period, pitch):
+    pieces = []
+    for m in range(first, first + rows, 8):
+        size = min(8, first + rows - m)
+        p, i = divmod(m, period)
+        for start, stop in ((i, min(i + size, period)), (period, i + size)):
+            if stop > start:
+                at = start % period * pitch + p + start // period
+                pieces.append(mid[tile, pl.ds(at, stop - start, stride=pitch), :])
+    return jnp.concatenate(pieces, axis=0)
+
+
+def matrix(mid, e, rows, width, pitch):
+    period = 3200 // width
+    tiles = [matrix_rows(mid, tile, e * rows, rows, period, pitch) for tile in range((width + 127) // 128)]
+    whole = tiles[0] if len(tiles) == 1 else jnp.concatenate(tiles, axis=1)
+    return whole[:, 0:width]
+
+
+def two_terms(rows):
+    high = rows.astype(BF16).astype(F32)
+    return jnp.concatenate([high, rows - high], axis=0).astype(BF16)
+
+
+def times_transposed(both, right):
+    out = lax.dot_general(both, right, (((1,), (1,)), ((), ())), preferred_element_type=F32)
+    return out[0:8] + out[8:16]
+
+
+def condense_body(
+    loads, inv_ref, cif_ref, cfi_ref, ff_ref, load_ref, fload_ref, count_ref,
+    condensed_ref, imap_ref, iload_ref, face_load_ref, blocks_ref,
+    flat_inv, flat_cif, flat_cfi, flat_ff, mid_inv, mid_cif, mid_cfi, mid_ff, wide,
+):
+    loads[0].wait()
+    squeeze(inv_ref, flat_inv)
+    loads[1].wait()
+    squeeze(cfi_ref, flat_cfi)
+    spread_rows(flat_inv, mid_inv, 100, 32, 33)
+    spread_rows(flat_cfi, mid_cfi, 100, 56, 57)
+    loads[2].wait()
+    squeeze(cif_ref, flat_cif)
+    loads[3].wait()
+    squeeze(ff_ref, flat_ff)
+    spread_rows(flat_cif, mid_cif, 200, 56, 57)
+    spread_rows(flat_ff, mid_ff, 200, 104, 105)
+    count = count_ref[0]
+    row100 = lax.broadcasted_iota(jnp.int32, (8, 100), 0)
+    row200 = lax.broadcasted_iota(jnp.int32, (8, 200), 0)
+    both = two_terms(load_ref[...])
+    iload = jnp.zeros((8, 100), F32)
+    for e in range(8):
+        inverse = matrix(mid_inv, e, 100, 100, 33).astype(BF16)
+        iload = jnp.where(row100 == e, times_transposed(both, inverse), iload)
+        inner = matrix(mid_cif, e, 100, 200, 57).astype(BF16)
+        imap_ref[e] = jnp.dot(inverse, inner, preferred_element_type=F32).astype(BF16)
+    iload_ref[...] = iload
+    both = two_terms(iload)
+    outer_load = jnp.zeros((8, 200), F32)
+    for e in range(8):
+        outer = matrix(mid_cfi, e, 200, 100, 57).astype(BF16)
+        outer_load = jnp.where(row200 == e, times_transposed(both, outer), outer_load)
+        product = jnp.dot(outer, imap_ref[e], preferred_element_type=F32)
+        alive = jnp.where(e < count, 1.0, 0.0)
+        block = ((matrix(mid_ff, e, 200, 200, 105) - product) * alive).astype(BF16)
+        condensed_ref[e] = block
+        block = block.astype(F32)
+        wide[0, 200 * e : 200 * e + 200, :] = block[:, 0:128]
+        wide[1, 200 * e : 200 * e + 200, :] = jnp.concatenate([block[:, 128:200], jnp.zeros((200, 56), F32)], axis=1)
+    face_load_ref[...] = jnp.where(row200 < count, fload_ref[...] - outer_load, 0.0)
+
+    lane = lax.broadcasted_iota(jnp.int32, (8, 128), 1)
+    for side in range(4):
+        start = DOF * side
+        tiles = [jnp.zeros((8, 128), F32) for _ in range(20)]
+        for i in range(DOF):
+            at = pl.ds(start + i, 8, stride=200)
+            if side == 2:
+                value = jnp.where(lane < 64, wide[1, at, :], wide[0, at, :])
+            else:
+                value = wide[start // 128, at, :]
+            tile, off = divmod(DOF * i, 128)
+            shift = (off - start) % 128
+            value = pltpu.roll(value, shift, 1) if shift else value
+            tiles[tile] = jnp.where((lane >= off) & (lane < off + DOF), value, tiles[tile])
+            if off + DOF > 128:
+                tiles[tile + 1] = jnp.where(lane < off + DOF - 128, value, tiles[tile + 1])
+        blocks_ref[8 * side : 8 * side + 8, :] = jnp.concatenate(tiles, axis=1).astype(BF16)
+
+
+def finish_kernel(trace_ref, state_ref, faces_ref, trace_out, state_out, faces_out):
+    trace_out[...] = trace_ref[:, 0:DOF]
+    state_out[...] = state_ref[:, 0:100]
+    faces_out[...] = faces_ref[:, 0 : DOF * DOF].astype(BF16)
 
 
 def per_device(
@@ -290,56 +407,64 @@
     inv_interior, couple_if, couple_fi, face_face, load_interior, load_face, jacobi_inverse,
     slot_face, send_slot, recv_face, partner_sub, elem_count,
 ):
-    elements = load_interior.shape[0]
-    interior = load_interior.shape[1]
-    face_width = load_face.shape[1]
-    face_count = jacobi_inverse.shape[0]
-    inv_interior, couple_if, couple_fi, face_face = squeezed(inv_interior, couple_if, couple_fi, face_face)
-    inverse_blocks = inv_interior.reshape(elements, interior, interior)
-    couple_in = couple_if.reshape(elements, interior, face_width)
-    couple_out = couple_fi.reshape(elements, face_width, interior)
-    face_block = face_face.reshape(elements, face_width, face_width)
-    living = (jnp.arange(elements, dtype=jnp.int32) < elem_count[0]).astype(F32)
-    interior_map = jnp.einsum(
-        "eij,ejk->eik", inverse_blocks, couple_in, preferred_element_type=F32
-    ).astype(BF16)
-    product = jnp.einsum("eij,ejk->eik", couple_out, interior_map, preferred_element_type=F32)
-    condensed = ((face_block.astype(F32) - product) * living[:, None, None]).astype(BF16)
-    interior_load = jnp.einsum(
-        "eij,ej->ei", inverse_blocks.astype(F32), load_interior, precision=HIGH
-    )
-    face_load = (
-        load_face - jnp.einsum("eij,ej->ei", couple_out.astype(F32), interior_load, precision=HIGH)
-    ) * living[:, None]
-    shaped = condensed.reshape(elements, 4, DOF, 4, DOF)
-    blocks = jnp.concatenate(
-        [shaped[:, side, :, side, :].reshape(elements, DOF * DOF) for side in range(4)], axis=0
-    )
-    blocks = jnp.pad(blocks, ((0, 0), (0, 60)))
     vmem = pl.BlockSpec(memory_space=pltpu.VMEM)
-    return pl.pallas_call(
+    smem = pl.BlockSpec(memory_space=pltpu.SMEM)
+    part = 2560 // CHUNKS
+    results = pl.pallas_call(
         functools.partial(exchange_kernel, doms, subs),
         out_shape=(
-            jax.ShapeDtypeStruct((face_count, DOF), F32),
-            jax.ShapeDtypeStruct((elements, interior), F32),
-            jax.ShapeDtypeStruct((face_count, DOF * DOF), BF16),
+            jax.ShapeDtypeStruct((24, 128), F32),
+            jax.ShapeDtypeStruct((8, 128), F32),
+            jax.ShapeDtypeStruct((24, 2560), F32),
         ),
-        in_specs=[pl.BlockSpec(memory_space=pltpu.SMEM)] * 4 + [vmem] * 7,
+        in_specs=[smem] * 5 + [pl.BlockSpec(memory_space=pl.ANY)] * 4 + [vmem] * 3,
         out_specs=(vmem, vmem, vmem),
         scratch_shapes=[
             pltpu.VMEM((24, 2688), F32),
             pltpu.VMEM((DOF, 24, 128), F32),
             pltpu.VMEM((6, 8, 128), F32),
             pltpu.VMEM((6, 32, 128), F32),
-            pltpu.VMEM((CHUNKS, GROUPS, 2, 2560 // CHUNKS), F32),
-            pltpu.VMEM((CHUNKS, 32, 2, 2560 // CHUNKS), F32),
+            pltpu.VMEM((CHUNKS, GROUPS, 2, part), F32),
+            pltpu.VMEM((CHUNKS, 32, 2, part), F32),
             pltpu.SemaphoreType.DMA((6,)),
             pltpu.SemaphoreType.DMA((6,)),
             pltpu.SemaphoreType.DMA((CHUNKS,)),
             pltpu.SemaphoreType.DMA((CHUNKS,)),
+            pltpu.VMEM(inv_interior.shape, BF16),
+            pltpu.VMEM(couple_if.shape, BF16),
+            pltpu.VMEM(couple_fi.shape, BF16),
+            pltpu.VMEM(face_face.shape, BF16),
+            pltpu.SemaphoreType.DMA((4,)),
+            pltpu.VMEM((8, 200, 200), BF16),
+            pltpu.VMEM((8, 100, 200), BF16),
+            pltpu.VMEM((8, 100), F32),
+            pltpu.VMEM((8, 200), F32),
+            pltpu.VMEM((32, 2560), BF16),
+            pltpu.VMEM((808, 128), F32),
+            pltpu.VMEM((1408, 128), F32),
+            pltpu.VMEM((1408, 128), F32),
+            pltpu.VMEM((2608, 128), F32),
+            pltpu.VMEM((1, 1064, 128), F32),
+            pltpu.VMEM((2, 920, 128), F32),
+            pltpu.VMEM((1, 1832, 128), F32),
+            pltpu.VMEM((2, 1688, 128), F32),
+            pltpu.VMEM((2, 1600, 128), F32),
         ],
         compiler_params=pltpu.CompilerParams(collective_id=0, has_side_effects=True),
-    )(slot_face.T, send_slot.transpose(0, 2, 1), recv_face.transpose(0, 2, 1), partner_sub, condensed, interior_map, interior_load, face_load, jacobi_inverse, blocks, living[:, None])
+    )(
+        slot_face.T, send_slot.transpose(0, 2, 1), recv_face.transpose(0, 2, 1), partner_sub, elem_count,
+        inv_interior, couple_if, couple_fi, face_face, load_interior, load_face, jacobi_inverse,
+    )
+    return pl.pallas_call(
+        finish_kernel,
+        out_shape=(
+            jax.ShapeDtypeStruct((24, DOF), F32),
+            jax.ShapeDtypeStruct((8, 100), F32),
+            jax.ShapeDtypeStruct((24, DOF * DOF), BF16),
+        ),
+        in_specs=[vmem] * 3,
+        out_specs=(vmem, vmem, vmem),
+    )(*results)
 
 
 def solution(mesh):

time: 83.9 us -> 60.5 us (0.72)
  local copies, waits for them, and re-layouts: 16.7 us -> 0 us
  matrix products: 2.73 us -> 0 us
  other arithmetic: 1.96 us -> 0 us
  Pallas kernels: 59.8 us -> 58.3 us
    convert_element_type x2 -> x0, local copies, waits for them, and re-layouts: 4.5 us -> none  [the longest x1 3.59 us: per_device(): face_block.astype(F32) - product]
    unnamed x17 -> x0, local copies, waits for them, and re-layouts: 4.17 us -> none
    reshape x4 -> x0, local copies, waits for them, and re-layouts: 3.53 us -> none  [the longest x1 1.57 us: per_device(): couple_out = couple_fi.reshape(elements, face_width, interior)]
    dot_general x4 -> x0, matrix products: 2.73 us -> none  [the longest x1 1.17 us: per_device(): jnp.einsum('eij,ejk->eik', inverse_blocks, couple_in, preferred_element_t...]
    slice x1 -> x0, local copies, waits for them, and re-layouts: 2.56 us -> none  [per_device(): shaped[:, side, :, side, :].reshape(elements, DOF * DOF)]
    pallas_call x1, Pallas kernels: 3.14 us -> 1.63 us  [per_device(): pl.pallas_call(finish_kernel, out_shape=(jax.ShapeDtypeStruct((24, DOF),...]
    dot_general x1 -> x0, local copies, waits for them, and re-layouts: 1.36 us -> none  [per_device(): jnp.einsum('eij,ejk->eik', inverse_blocks, couple_in, preferred_element_t...]
where the time goes in v3:
time: 60.5 us; the launch traced here: 59.5 us
  Pallas kernels  58.3 us (96%)
  between operations  1.29 us (2%)
    pallas_call x1, Pallas kernels, per_device(): pl.pallas_call(functools.partial(exchange_kernel, doms, subs), out_shape=...  56.6 us
    pallas_call x1, Pallas kernels, per_device(): pl.pallas_call(finish_kernel, out_shape=(jax.ShapeDtypeStruct((24, DOF),...  1.63 us

profile of v3, /device:TPU:1, one launch (start us, length us, event | category | flops | bytes accessed | tf_op | source)
XLA Modules:
  0.0 59.5 jit_solution(1580527238744837580)
XLA Ops:
  1.3 56.6 %shard_map.139 = (f32[24,128]{1,0:T(8,128)}, f32[8,128]{1,0:T(8,128)}, f32[24,2560]{1,0:T(8,128)}) custom-call(s32[4,8]{1,0:T(4,128)} %bitcast.3, s32[1,2,4]{2,1,0:T(2,128)} %bitcast.4, s32[1,2,4]{2,1,0:T(2,128)} %bitcast.5, s32[1,8]{1,0:T(1,128)} %partner_ref.1, s32[1]{0:T(128)S(6)} %copy.15.count_ref, bf16[1,80000]{1,0:T(2,128)(2,1)} %inv_hbm.1, ...), custom_call_target="tpu_custom_call" | custom-call | tf_op jit(solution)/shard_map/pallas_call | solution.py:413
  57.9 1.6 %shard_map.140 = (f32[24,50]{1,0:T(8,128)}, f32[8,100]{1,0:T(8,128)}, bf16[24,2500]{1,0:T(8,128)(2,1)}) custom-call(f32[24,128]{1,0:T(8,128)} %get-tuple-element.6.trace_ref, f32[8,128]{1,0:T(8,128)} %get-tuple-element.7.state_ref, f32[24,2560]{1,0:T(8,128)} %get-tuple-element.8.faces_ref), custom_call_target="tpu_custom_call" | custom-call | tf_op jit(solution)/shard_map/pallas_call | solution.py:458

commit v4 on v3

--- a/solution.py
+++ b/solution.py
@@ -19,6 +19,10 @@
     return [0, 1, doms // 2, doms - 1][group]
 
 
+def far_first(step):
+    return 4 + (step + 1) // 2 * (2 * (step % 2) - 1)
+
+
 def split_dot(left, right):
     high = right.astype(BF16)
     low = (right - high.astype(F32)).astype(BF16)
@@ -29,41 +33,47 @@
 
 def exchange_kernel(
     doms, subs,
-    slot_ref, send_ref, recv_ref, partner_ref, count_ref,
-    inv_hbm, cif_hbm, cfi_hbm, ff_hbm, load_ref, fload_ref, jac_ref,
+    slot_hbm, send_hbm, recv_hbm, partner_hbm, count_hbm,
+    inv_hbm, cif_hbm, cfi_hbm, ff_hbm, load_hbm, fload_hbm, jac_hbm,
     trace_ref, state_ref, faces_ref,
     jflat, jrows, sbuf, rbuf, sbig, rbig, send_sem, recv_sem, bsend_sem, brecv_sem,
-    inv_ref, cif_ref, cfi_ref, ff_ref, in_sem, condensed_ref, imap_ref, iload_ref, face_load_ref, blocks_ref,
+    inv_ref, cif_ref, cfi_ref, ff_ref, load_ref, fload_ref, jac_ref,
+    slot_ref, send_ref, recv_ref, partner_ref, count_ref, in_sem, condensed_ref, imap_ref, iload_ref, face_load_ref, blocks_ref,
     *spaces,
 ):
     dom, sub = lax.axis_index("dom"), lax.axis_index("sub")
+    offsets = [group_offset(g, doms) for g in range(GROUPS)]
+    barrier = pltpu.get_barrier_semaphore()
+
+    def greet(step, carry):
+        for g in (2, 1, 3, 0):
+            other = lax.rem(sub + far_first(step), subs)
+            target = lax.rem(dom + offsets[g], doms)
+
+            def signal():
+                pl.semaphore_signal(barrier, inc=1, device_id=(target, other), device_id_type=pl.DeviceIdType.MESH)
+
+            if g == 0:
+                pl.when(step < subs - 1)(signal)
+            else:
+                signal()
+        return carry
+
     loads = [
         pltpu.make_async_copy(source, target, in_sem.at[k])
         for k, (source, target) in enumerate(
-            ((inv_hbm, inv_ref), (cfi_hbm, cfi_ref), (cif_hbm, cif_ref), (ff_hbm, ff_ref))
+            (
+                (inv_hbm, inv_ref), (cfi_hbm, cfi_ref), (cif_hbm, cif_ref), (ff_hbm, ff_ref),
+                (load_hbm, load_ref), (fload_hbm, fload_ref), (jac_hbm, jac_ref),
+                (slot_hbm, slot_ref), (send_hbm, send_ref), (recv_hbm, recv_ref),
+                (partner_hbm, partner_ref), (count_hbm, count_ref),
+            )
         )
     ]
     for load in loads:
         load.start()
-    offsets = [group_offset(g, doms) for g in range(GROUPS)]
     for phase in range(6):
         rbuf[phase] = jnp.zeros(rbuf.shape[1:], F32)
-    barrier = pltpu.get_barrier_semaphore()
-
-    def greet(step, carry):
-        for g in range(GROUPS):
-            other = lax.rem(sub + step, subs)
-            target = lax.rem(dom + offsets[g], doms)
-
-            def signal():
-                pl.semaphore_signal(barrier, inc=1, device_id=(target, other), device_id_type=pl.DeviceIdType.MESH)
-
-            if g == 0:
-                pl.when(step > 0)(signal)
-            else:
-                signal()
-        return carry
-
     lax.fori_loop(0, subs, greet, 0)
 
     condense_body(
@@ -71,6 +81,7 @@
         condensed_ref, imap_ref, iload_ref, face_load_ref, blocks_ref, *spaces,
     )
 
+    loads[6].wait()
     jflat[:, 0:2500] = jac_ref[...].astype(F32)
     jflat[:, 2500:2688] = jnp.zeros((24, 188), F32)
     for i in range(DOF):
@@ -97,8 +108,8 @@
         sbuf[phase] = rows
 
         def body(step, carry):
-            other = lax.rem(sub + step, subs)
-            for g in range(GROUPS):
+            other = lax.rem(sub + far_first(step), subs)
+            for g in (2, 1, 3, 0):
                 target = lax.rem(dom + (doms - offsets[g] if sign < 0 else offsets[g]), doms)
 
                 def go():
@@ -112,7 +123,7 @@
                     ).start()
 
                 if g == 0:
-                    pl.when(step > 0)(go)
+                    pl.when(step < subs - 1)(go)
                 else:
                     go()
             return carry
@@ -128,8 +139,8 @@
         width = 2560 // CHUNKS
 
         def body(step, carry):
-            other = lax.rem(sub + step, subs)
-            for g in range(GROUPS):
+            other = lax.rem(sub + far_first(step), subs)
+            for g in (2, 1, 3, 0):
                 target = lax.rem(dom + doms - offsets[g], doms)
 
                 def go():
@@ -143,7 +154,7 @@
                     ).start()
 
                 if g == 0:
-                    pl.when(step > 0)(go)
+                    pl.when(step < subs - 1)(go)
                 else:
                     go()
             return carry
@@ -352,9 +363,13 @@
     squeeze(ff_ref, flat_ff)
     spread_rows(flat_cif, mid_cif, 200, 56, 57)
     spread_rows(flat_ff, mid_ff, 200, 104, 105)
+    for load in loads[7:]:
+        load.wait()
     count = count_ref[0]
     row100 = lax.broadcasted_iota(jnp.int32, (8, 100), 0)
     row200 = lax.broadcasted_iota(jnp.int32, (8, 200), 0)
+    loads[4].wait()
+    loads[5].wait()
     both = two_terms(load_ref[...])
     iload = jnp.zeros((8, 100), F32)
     for e in range(8):
@@ -396,19 +411,341 @@
         blocks_ref[8 * side : 8 * side + 8, :] = jnp.concatenate(tiles, axis=1).astype(BF16)
 
 
+def slots_of(wide):
+    lane = lax.broadcasted_iota(jnp.int32, (8, 128), 1)
+    pieces = []
+    for side in range(4):
+        turned = wide if side == 0 else pltpu.roll(wide, 256 - DOF * side, 1)
+        pieces.append(jnp.where(lane < DOF, turned[:, 0:128], 0.0))
+    return jnp.concatenate(pieces, axis=0)
+
+
+def elements_of(slots):
+    zero = jnp.zeros((8, 128), F32)
+    total = jnp.concatenate([slots[0:8], zero], axis=1)
+    for side in range(1, 4):
+        wide = jnp.concatenate([slots[8 * side : 8 * side + 8], zero], axis=1)
+        total = total + pltpu.roll(wide, DOF * side, 1)
+    return total
+
+
+def each_element(elements, matrix_ref, rows):
+    both = two_terms(elements)[:, 0:200]
+    row = lax.broadcasted_iota(jnp.int32, (8, rows), 0)
+    total = jnp.zeros((8, rows), F32)
+    for e in range(8):
+        total = jnp.where(row == e, times_transposed(both, matrix_ref[e]), total)
+    return total
+
+
+def twice(rows):
+    return jnp.concatenate([rows, pltpu.roll(rows, 64, 1)], axis=0)
+
+
+MIRROR = (0, 3, 2, 1)
+
+
+def virtual_hots(slot_ref, send_ref, recv_ref, partner_ref, subs):
+    lane = lax.broadcasted_iota(jnp.int32, (8, 128), 1)
+    row = lax.broadcasted_iota(jnp.int32, (8, 128), 0)
+    row24 = lax.broadcasted_iota(jnp.int32, (24, 128), 0)
+    row32 = lax.broadcasted_iota(jnp.int32, (32, 128), 0)
+    nothing = jnp.full((8, 128), -1000, jnp.int32)
+    no = jnp.zeros((8, 128), F32)
+    faces, slots = {}, {}
+    for g in range(GROUPS):
+        for r in range(2):
+            face, slot = recv_ref[0, r, g], send_ref[0, r, g]
+            faces[g, r] = jnp.where(face < 24, face, -1000)
+            slots[g, r] = jnp.where(slot < 32, (slot & 3) * 8 + (slot >> 2), -1000)
+    table_l, columns = nothing, []
+    for side in range(4):
+        column = nothing
+        for e in range(8):
+            face = slot_ref[side, e]
+            face = jnp.where(face < 24, face, -1000)
+            table_l = jnp.where(lane == 8 * side + e, face, table_l)
+            column = jnp.where(row == e, face, column)
+        columns.append(column)
+    table_e, table_d, table_f = nothing, nothing, nothing
+    hot_g, hot_r, hot_j, pick = no, no, no, [no, no]
+    for g in range(GROUPS):
+        holder, owner = partner_ref[0, g], partner_ref[0, GROUPS + g]
+        mirror = MIRROR[g]
+        for r in range(2):
+            face, slot, rank = faces[g, r], slots[g, r], 24 + 2 * g + r
+            table_l = jnp.where(lane == slot, rank, table_l)
+            columns = [jnp.where(row + 8 * side == slot, rank, column) for side, column in enumerate(columns)]
+            alive = jnp.where(slot >= 0, rank, -1000)
+            table_e = jnp.where(lane == 64 * r + 2 * (subs * g + owner), alive, table_e)
+            table_e = jnp.where(lane == 64 * r + 2 * (subs * mirror + holder) + 1, face, table_e)
+            table_d = jnp.where(lane == 32 * r + subs * g + owner, alive, table_d)
+            table_f = jnp.where(lane == 2 * g + r, face, table_f)
+            hot_g = jnp.where((row == g) & (lane == 24 * r + face), 1.0, hot_g)
+            hot_r = jnp.where((row == 2 * g + r) & (lane == slot), 1.0, hot_r)
+            hot_j = jnp.where((row == 2 * g + r) & (lane == face), 1.0, hot_j)
+            pick[r] = jnp.where((row == 2 * g) & (lane == face), 1.0, pick[r])
+            pick[r] = jnp.where((row == 2 * mirror + 1) & (lane == rank), 1.0, pick[r])
+
+    def equal(rows, table):
+        return (rows == jnp.concatenate([table] * (rows.shape[0] // 8), axis=0)).astype(F32)
+
+    hot_x = jnp.concatenate([(lane == column).astype(F32) for column in columns], axis=0)
+    local = equal(row32, table_l).astype(BF16)
+    sent = [jnp.dot(part.astype(BF16)[:, 0:32], local, preferred_element_type=F32) for part in pick]
+    hot_s = sent[0] + pltpu.roll(sent[1], 32, 1)
+    twins = jnp.int32(0)
+    flat = [faces[g, r] for g in range(GROUPS) for r in range(2)]
+    for k, face in enumerate(flat):
+        for other in flat[:k]:
+            twins = twins + jnp.where(face == other, jnp.where(face >= 0, 1, 0), 0)
+    hots = (hot_s, hot_x, equal(row32, table_e), equal(row32, table_d), hot_g, hot_r, hot_j, equal(row24, table_f))
+    return (local,) + tuple(hot.astype(BF16) for hot in hots) + (twins,)
+
+
+def sweep_kernel(
+    doms, subs,
+    slot_hbm, send_hbm, recv_hbm, partner_hbm, count_hbm,
+    inv_hbm, cif_hbm, cfi_hbm, ff_hbm, load_hbm, fload_hbm, jac_hbm,
+    trace_ref, state_ref, faces_ref, twins_ref,
+    jflat, jrows, esend, ebuf, dsend, dbuf, fsend, fbuf, bsend, bbuf, jsend, jbuf,
+    esend_sem, erecv_sem, dsend_sem, drecv_sem, fsend_sem, frecv_sem, bsend_sem, brecv_sem, jsend_sem, jrecv_sem,
+    inv_ref, cif_ref, cfi_ref, ff_ref, load_ref, fload_ref, jac_ref,
+    slot_ref, send_ref, recv_ref, partner_ref, count_ref, in_sem,
+    condensed_ref, imap_ref, iload_ref, face_load_ref, blocks_ref,
+    *spaces,
+):
+    dom, sub = lax.axis_index("dom"), lax.axis_index("sub")
+    mesh_ids = pl.DeviceIdType.MESH
+    offsets = [group_offset(g, doms) for g in range(GROUPS)]
+    barrier = pltpu.get_barrier_semaphore()
+    rank, block = lax.rem(dom, 8), dom // 8
+
+    def hello(target, other):
+        pl.semaphore_signal(barrier, inc=1, device_id=(target, other), device_id_type=mesh_ids)
+
+    def to_all(start):
+        def body(step, carry):
+            other = lax.rem(sub + far_first(step), subs)
+            for g in (2, 1, 3, 0):
+                target = lax.rem(dom + offsets[g], doms)
+                if g == 0:
+                    pl.when(step < subs - 1)(functools.partial(start, g, target, other))
+                else:
+                    start(g, target, other)
+            return carry
+
+        lax.fori_loop(0, subs, body, 0)
+
+    stages = (
+        lambda step: (dom, lax.rem(sub + step, subs)),
+        lambda step: (lax.rem(dom + 8 * step, doms), sub),
+        lambda step: (8 * block + lax.rem(rank + step, 8), sub),
+    )
+    places = (sub, block, rank)
+    for phase in range(3):
+        ebuf[phase] = jnp.zeros(ebuf.shape[1:], F32)
+        fbuf[phase] = jnp.zeros(fbuf.shape[1:], F32)
+    dbuf[...] = jnp.zeros(dbuf.shape, F32)
+    to_all(lambda g, target, other: hello(target, other))
+
+    def more(step, carry):
+        hello(*stages[1](step))
+        hello(*stages[2](step))
+        return carry
+
+    lax.fori_loop(1, 8, more, 0)
+    loads = [
+        pltpu.make_async_copy(source, target, in_sem.at[k])
+        for k, (source, target) in enumerate(
+            (
+                (inv_hbm, inv_ref), (cfi_hbm, cfi_ref), (cif_hbm, cif_ref), (ff_hbm, ff_ref),
+                (load_hbm, load_ref), (fload_hbm, fload_ref), (jac_hbm, jac_ref),
+                (slot_hbm, slot_ref), (send_hbm, send_ref), (recv_hbm, recv_ref),
+                (partner_hbm, partner_ref), (count_hbm, count_ref),
+            )
+        )
+    ]
+    for load in loads:
+        load.start()
+    condense_body(
+        loads, inv_ref, cif_ref, cfi_ref, ff_ref, load_ref, fload_ref, count_ref,
+        condensed_ref, imap_ref, iload_ref, face_load_ref, blocks_ref, *spaces,
+    )
+    local, hot_s, hot_x, hot_e, hot_d, hot_g, hot_r, hot_j, hot_f, twins = virtual_hots(
+        slot_ref, send_ref, recv_ref, partner_ref, subs
+    )
+
+    def fill_rows(first, rows):
+        for i in range(DOF):
+            start = DOF * i
+            base = min(start // 128 * 128, 2432)
+            window = jflat[first : first + rows, base : base + 256]
+            jrows[i, first : first + rows, :] = pltpu.roll(window, 256 - (start - base), 1)[:, 0:128]
+
+    loads[6].wait()
+    jflat[0:24, 0:2500] = jac_ref[...].astype(F32)
+    jflat[:, 2500:2688] = jnp.zeros((32, 188), F32)
+    jflat[24:32, 0:2500] = jnp.zeros((8, 2500), F32)
+    for i in range(DOF):
+        jrows[i, 24:32, :] = jnp.zeros((8, 128), F32)
+    fill_rows(0, 24)
+    part = 2560 // CHUNKS
+    inverses = jflat[0:24, 0:2560].astype(BF16)
+    blocks = blocks_ref[...]
+    picked_j = jnp.dot(hot_j[:, 0:24], inverses, preferred_element_type=F32)
+    picked_b = jnp.dot(hot_r[:, 0:32], blocks, preferred_element_type=F32)
+    for chunk in range(CHUNKS):
+        for g in range(GROUPS):
+            jsend[chunk, g] = picked_j[2 * g : 2 * g + 2, chunk * part : (chunk + 1) * part]
+            bsend[chunk, MIRROR[g]] = picked_b[2 * g : 2 * g + 2, chunk * part : (chunk + 1) * part]
+    lane32 = lax.broadcasted_iota(jnp.int32, (32, 128), 1)
+
+    def short(rows):
+        return jnp.where(lane32 < DOF, rows, 0.0)
+
+    def jacobi(vector):
+        total = jnp.zeros((32, 128), F32)
+        for i in range(DOF):
+            entry = jnp.sum(jrows[i] * vector, axis=1, keepdims=True)
+            total = jnp.where(lane32 == i, entry, total)
+        return total
+
+    def start_swap(phase, slots):
+        esend[phase] = split_dot(hot_s[:, 0:64], twice(slots))
+
+        def start(g, target, other):
+            pltpu.make_async_remote_copy(
+                src_ref=esend.at[phase, pl.ds(2 * g, 2)],
+                dst_ref=ebuf.at[phase, pl.ds(2 * (g * subs + sub), 2)],
+                send_sem=esend_sem.at[phase], recv_sem=erecv_sem.at[phase],
+                device_id=(target, other), device_id_type=mesh_ids,
+            ).start()
+
+        to_all(start)
+
+    def finish_swap(phase, slots):
+        own = split_dot(local[:, 0:32], slots)
+        whole = ebuf.at[phase, pl.ds(0, 62)]
+        pltpu.make_async_copy(whole, whole, erecv_sem.at[phase]).wait()
+        return short(own + split_dot(hot_e, twice(ebuf[phase])))
+
+    def start_stage(stage, value):
+        fsend[stage] = value
+
+        def body(step, carry):
+            pltpu.make_async_remote_copy(
+                src_ref=fsend.at[stage, pl.ds(0, 1)], dst_ref=fbuf.at[stage, pl.ds(places[stage], 1)],
+                send_sem=fsend_sem.at[stage], recv_sem=frecv_sem.at[stage],
+                device_id=stages[stage](step), device_id_type=mesh_ids,
+            ).start()
+            return carry
+
+        lax.fori_loop(1, 8, body, 0)
+
+    def finish_stage(stage, value):
+        whole = fbuf.at[stage, pl.ds(0, 7)]
+        pltpu.make_async_copy(whole, whole, frecv_sem.at[stage]).wait()
+        return value + jnp.sum(fbuf[stage], axis=0, keepdims=True)
+
+    def start_chunks(source, target_ref, send_sem, recv_sem, first, last):
+        for chunk in range(first, last):
+
+            def start(g, target, other):
+                pltpu.make_async_remote_copy(
+                    src_ref=source.at[chunk, g], dst_ref=target_ref.at[chunk, g * subs + sub],
+                    send_sem=send_sem.at[chunk], recv_sem=recv_sem.at[chunk],
+                    device_id=(target, other), device_id_type=mesh_ids,
+                ).start()
+
+            to_all(start)
+
+    def finish_chunks(target_ref, recv_sem, index):
+        for chunk in range(CHUNKS):
+            whole = target_ref.at[chunk, pl.ds(0, 31)]
+            pltpu.make_async_copy(whole, whole, recv_sem.at[chunk]).wait()
+        rows = [
+            jnp.concatenate([target_ref[chunk, index(g)] for chunk in range(CHUNKS)], axis=1) for g in range(GROUPS)
+        ]
+        return jnp.concatenate(rows, axis=0)
+
+    start_jac = functools.partial(start_chunks, jsend, jbuf, jsend_sem, jrecv_sem)
+    start_blocks = functools.partial(start_chunks, bsend, bbuf, bsend_sem, brecv_sem)
+    found = jnp.zeros((8, 128), F32) + twins.astype(F32)
+
+    def padded(rows):
+        return jnp.concatenate([rows, jnp.zeros((8, 56), F32)], axis=1)
+
+    slots = slots_of(padded(face_load_ref[...]))
+    pl.semaphore_wait(barrier, 45)
+    start_swap(0, slots)
+    start_stage(0, found)
+    start_jac(0, 3)
+    rhs = finish_swap(0, slots)
+    found = finish_stage(0, found)
+    traces = jacobi(rhs)
+
+    dsend[...] = split_dot(hot_g[:, 0:48], twice(traces[0:24]))
+
+    def start_trace(g, target, other):
+        pltpu.make_async_remote_copy(
+            src_ref=dsend.at[pl.ds(g, 1)], dst_ref=dbuf.at[pl.ds(g * subs + sub, 1)],
+            send_sem=dsend_sem, recv_sem=drecv_sem, device_id=(target, other), device_id_type=mesh_ids,
+        ).start()
+
+    to_all(start_trace)
+    start_stage(1, found)
+    start_jac(3, 5)
+    start_blocks(0, 1)
+    pltpu.make_async_copy(dbuf.at[pl.ds(0, 31)], dbuf.at[pl.ds(0, 31)], drecv_sem).wait()
+    traces = short(traces + split_dot(hot_d[:, 0:64], twice(dbuf[...])))
+    found = finish_stage(1, found)
+
+    for sweep in range(SWEEPS):
+        elements = elements_of(short(split_dot(hot_x[:, 0:32], traces)))
+        slots = slots_of(padded(each_element(elements, condensed_ref, 200)))
+        start_swap(1 + sweep, slots)
+        start_blocks(1 + 2 * sweep, 3 + 2 * sweep)
+        if sweep == 0:
+            start_stage(2, found)
+        total = finish_swap(1 + sweep, slots)
+        if sweep == 0:
+            jflat[24:32, 0:2560] = finish_chunks(jbuf, jrecv_sem, lambda g: g * subs + partner_ref[0, GROUPS + g])
+            fill_rows(24, 8)
+        traces = traces + jacobi(rhs - total)
+    twins_ref[...] = jnp.where(finish_stage(2, found)[0:1, 0:1] > 0.0, 1, 0)
+    trace_ref[...] = traces[0:24]
+    elements = elements_of(short(split_dot(hot_x[:, 0:32], traces)))
+    row100 = lax.broadcasted_iota(jnp.int32, (8, 100), 0)
+    state = iload_ref[...] - each_element(elements, imap_ref, 100)
+    state = jnp.where(row100 < count_ref[0], state, 0.0)
+    state_ref[...] = jnp.concatenate([state, jnp.zeros((8, 28), F32)], axis=1)
+    sums = jnp.dot(local[0:24, 0:32], blocks, preferred_element_type=F32)
+    far = finish_chunks(bbuf, brecv_sem, lambda g: MIRROR[g] * subs + partner_ref[0, g]).astype(BF16)
+    faces_ref[...] = sums + jnp.dot(hot_f[:, 0:8], far, preferred_element_type=F32)
+    for phase in range(3):
+        pltpu.make_async_copy(ebuf.at[phase, pl.ds(0, 62)], ebuf.at[phase, pl.ds(0, 62)], esend_sem.at[phase]).wait()
+        pltpu.make_async_copy(fbuf.at[phase, pl.ds(0, 7)], fbuf.at[phase, pl.ds(0, 7)], fsend_sem.at[phase]).wait()
+    pltpu.make_async_copy(dbuf.at[pl.ds(0, 31)], dbuf.at[pl.ds(0, 31)], dsend_sem).wait()
+    for chunk in range(CHUNKS):
+        whole = bbuf.at[chunk, pl.ds(0, 31)]
+        pltpu.make_async_copy(whole, whole, bsend_sem.at[chunk]).wait()
+        whole = jbuf.at[chunk, pl.ds(0, 31)]
+        pltpu.make_async_copy(whole, whole, jsend_sem.at[chunk]).wait()
+
+
 def finish_kernel(trace_ref, state_ref, faces_ref, trace_out, state_out, faces_out):
     trace_out[...] = trace_ref[:, 0:DOF]
     state_out[...] = state_ref[:, 0:100]
     faces_out[...] = faces_ref[:, 0 : DOF * DOF].astype(BF16)
 
 
-def per_device(
+def six_exchanges(
     doms, subs,
     inv_interior, couple_if, couple_fi, face_face, load_interior, load_face, jacobi_inverse,
     slot_face, send_slot, recv_face, partner_sub, elem_count,
 ):
     vmem = pl.BlockSpec(memory_space=pltpu.VMEM)
-    smem = pl.BlockSpec(memory_space=pltpu.SMEM)
     part = 2560 // CHUNKS
     results = pl.pallas_call(
         functools.partial(exchange_kernel, doms, subs),
@@ -417,7 +754,7 @@
             jax.ShapeDtypeStruct((8, 128), F32),
             jax.ShapeDtypeStruct((24, 2560), F32),
         ),
-        in_specs=[smem] * 5 + [pl.BlockSpec(memory_space=pl.ANY)] * 4 + [vmem] * 3,
+        in_specs=[pl.BlockSpec(memory_space=pl.ANY)] * 12,
         out_specs=(vmem, vmem, vmem),
         scratch_shapes=[
             pltpu.VMEM((24, 2688), F32),
@@ -430,31 +767,49 @@
             pltpu.SemaphoreType.DMA((6,)),
             pltpu.SemaphoreType.DMA((CHUNKS,)),
             pltpu.SemaphoreType.DMA((CHUNKS,)),
-            pltpu.VMEM(inv_interior.shape, BF16),
-            pltpu.VMEM(couple_if.shape, BF16),
-            pltpu.VMEM(couple_fi.shape, BF16),
-            pltpu.VMEM(face_face.shape, BF16),
-            pltpu.SemaphoreType.DMA((4,)),
-            pltpu.VMEM((8, 200, 200), BF16),
-            pltpu.VMEM((8, 100, 200), BF16),
-            pltpu.VMEM((8, 100), F32),
-            pltpu.VMEM((8, 200), F32),
-            pltpu.VMEM((32, 2560), BF16),
-            pltpu.VMEM((808, 128), F32),
-            pltpu.VMEM((1408, 128), F32),
-            pltpu.VMEM((1408, 128), F32),
-            pltpu.VMEM((2608, 128), F32),
-            pltpu.VMEM((1, 1064, 128), F32),
-            pltpu.VMEM((2, 920, 128), F32),
-            pltpu.VMEM((1, 1832, 128), F32),
-            pltpu.VMEM((2, 1688, 128), F32),
-            pltpu.VMEM((2, 1600, 128), F32),
-        ],
-        compiler_params=pltpu.CompilerParams(collective_id=0, has_side_effects=True),
+        ] + local_scratch(inv_interior, couple_if, couple_fi, face_face),
+        compiler_params=pltpu.CompilerParams(collective_id=1, has_side_effects=True),
     )(
         slot_face.T, send_slot.transpose(0, 2, 1), recv_face.transpose(0, 2, 1), partner_sub, elem_count,
         inv_interior, couple_if, couple_fi, face_face, load_interior, load_face, jacobi_inverse,
     )
+    return finish(results)
+
+
+def local_scratch(inv_interior, couple_if, couple_fi, face_face):
+    return [
+        pltpu.VMEM(inv_interior.shape, BF16),
+        pltpu.VMEM(couple_if.shape, BF16),
+        pltpu.VMEM(couple_fi.shape, BF16),
+        pltpu.VMEM(face_face.shape, BF16),
+        pltpu.VMEM((8, 100), F32),
+        pltpu.VMEM((8, 200), F32),
+        pltpu.VMEM((24, 2500), BF16),
+        pltpu.SMEM((4, 8), jnp.int32),
+        pltpu.SMEM((1, 2, 4), jnp.int32),
+        pltpu.SMEM((1, 2, 4), jnp.int32),
+        pltpu.SMEM((1, 8), jnp.int32),
+        pltpu.SMEM((1,), jnp.int32),
+        pltpu.SemaphoreType.DMA((12,)),
+        pltpu.VMEM((8, 200, 200), BF16),
+        pltpu.VMEM((8, 100, 200), BF16),
+        pltpu.VMEM((8, 100), F32),
+        pltpu.VMEM((8, 200), F32),
+        pltpu.VMEM((32, 2560), BF16),
+        pltpu.VMEM((808, 128), F32),
+        pltpu.VMEM((1408, 128), F32),
+        pltpu.VMEM((1408, 128), F32),
+        pltpu.VMEM((2608, 128), F32),
+        pltpu.VMEM((1, 1064, 128), F32),
+        pltpu.VMEM((2, 920, 128), F32),
+        pltpu.VMEM((1, 1832, 128), F32),
+        pltpu.VMEM((2, 1688, 128), F32),
+        pltpu.VMEM((2, 1600, 128), F32),
+    ]
+
+
+def finish(results):
+    vmem = pl.BlockSpec(memory_space=pltpu.VMEM)
     return pl.pallas_call(
         finish_kernel,
         out_shape=(
@@ -467,6 +822,53 @@
     )(*results)
 
 
+def per_device(doms, subs, *arrays):
+    vmem = pl.BlockSpec(memory_space=pltpu.VMEM)
+    part = 2560 // CHUNKS
+    loads, tables = arrays[:7], arrays[7:]
+    slot_face, send_slot, recv_face, partner_sub, elem_count = tables
+    *results, twins = pl.pallas_call(
+        functools.partial(sweep_kernel, doms, subs),
+        out_shape=(
+            jax.ShapeDtypeStruct((24, 128), F32),
+            jax.ShapeDtypeStruct((8, 128), F32),
+            jax.ShapeDtypeStruct((24, 2560), F32),
+            jax.ShapeDtypeStruct((1, 1), jnp.int32),
+        ),
+        in_specs=[pl.BlockSpec(memory_space=pl.ANY)] * 12,
+        out_specs=(vmem, vmem, vmem, vmem),
+        scratch_shapes=[
+            pltpu.VMEM((32, 2688), F32),
+            pltpu.VMEM((DOF, 32, 128), F32),
+            pltpu.VMEM((3, 8, 128), F32),
+            pltpu.VMEM((3, 64, 128), F32),
+            pltpu.VMEM((8, 128), F32),
+            pltpu.VMEM((32, 128), F32),
+            pltpu.VMEM((3, 8, 128), F32),
+            pltpu.VMEM((3, 8, 128), F32),
+            pltpu.VMEM((CHUNKS, GROUPS, 2, part), F32),
+            pltpu.VMEM((CHUNKS, 32, 2, part), F32),
+            pltpu.VMEM((CHUNKS, GROUPS, 2, part), F32),
+            pltpu.VMEM((CHUNKS, 32, 2, part), F32),
+            pltpu.SemaphoreType.DMA((3,)),
+            pltpu.SemaphoreType.DMA((3,)),
+            pltpu.SemaphoreType.DMA,
+            pltpu.SemaphoreType.DMA,
+            pltpu.SemaphoreType.DMA((3,)),
+            pltpu.SemaphoreType.DMA((3,)),
+            pltpu.SemaphoreType.DMA((CHUNKS,)),
+            pltpu.SemaphoreType.DMA((CHUNKS,)),
+            pltpu.SemaphoreType.DMA((CHUNKS,)),
+            pltpu.SemaphoreType.DMA((CHUNKS,)),
+        ] + local_scratch(*loads[:4]),
+        compiler_params=pltpu.CompilerParams(collective_id=0, has_side_effects=True, vmem_limit_bytes=67043328),
+    )(slot_face.T, send_slot.transpose(0, 2, 1), recv_face.transpose(0, 2, 1), partner_sub, elem_count, *loads)
+    return lax.switch(
+        twins.reshape(()),
+        (lambda: finish(results), lambda: six_exchanges(doms, subs, *arrays)),
+    )
+
+
 def solution(mesh):
     rows = P(("dom", "sub"), None)
     placed = (rows,) * 8 + (P(("dom", "sub"), None, None),) * 2 + (rows, P(("dom", "sub")))

time: 60.5 us -> 57.2 us (0.945); the launches traced: 59.5 us -> 57 us
  Pallas kernels: 58.3 us -> 55.1 us
    pallas_call x2, Pallas kernels: 58.3 us -> 55.1 us  [the longest x1 53.5 us: per_device(): pl.pallas_call(functools.partial(sweep_kernel, doms, subs), out_shape=(ja...]
where the time goes in v4:
time: 57.2 us; the launch traced here: 57 us
  Pallas kernels  55.1 us (96%)
  between operations  1.84 us (3%)
    pallas_call x1, Pallas kernels, per_device(): pl.pallas_call(functools.partial(sweep_kernel, doms, subs), out_shape=(ja...  53.5 us
    pallas_call x1, Pallas kernels, finish(): pl.pallas_call(finish_kernel, out_shape=(jax.ShapeDtypeStruct((24, DOF),...  1.63 us

profile of v4, /device:TPU:1, one launch (start us, length us, event | category | flops | bytes accessed | tf_op | source)
XLA Modules:
  0.0 57.0 jit_solution(137988485520646934)
XLA Ops:
  1.3 53.5 %shard_map.145 = (f32[24,128]{1,0:T(8,128)}, f32[8,128]{1,0:T(8,128)}, f32[24,2560]{1,0:T(8,128)}, s32[1,1]{1,0:T(1,128)}) custom-call(s32[4,8]{1,0:T(4,128)} %bitcast.7, s32[1,2,4]{2,1,0:T(2,128)} %bitcast.9, s32[1,2,4]{2,1,0:T(2,128)} %bitcast.11, s32[1,8]{1,0:T(1,128)} %partner_hbm.1, s32[1]{0:T(128)S(6)} %copy.27.count_hbm, bf16[1,80000]{1,0:T(2,128)(2,1)} %inv_hbm.1, ...), custom_call_target="tpu_custom_call" | custom-call | tf_op jit(solution)/shard_map/pallas_call | solution.py:830
  55.3 1.6 %conditional.1 = ((f32[24,50]{1,0:T(8,128)}, f32[8,100]{1,0:T(8,128)}, bf16[24,2500]{1,0:T(8,128)(2,1)})) conditional(s32[]{:T(128)} %bitcast.6, (f32[24,128]{1,0:T(8,128)}, f32[8,128]{1,0:T(8,128)}, f32[24,2560]{1,0:T(8,128)}) %tuple.13, (s32[8,4]{0,1:T(4,128)}, s32[1,4,2]{1,2,0:T(2,128)}, s32[1,4,2]{1,2,0:T(2,128)}, s32[1,8]{1,0:T(1,128)}, ...), branch_computations={%region_0.0_spmd, %region_1.0_spmd} | conditional | bytes 8 | solution.py:866
  55.4 1.6 %branch_0_fun.1 = (f32[24,50]{1,0:T(8,128)}, f32[8,100]{1,0:T(8,128)}, bf16[24,2500]{1,0:T(8,128)(2,1)}) custom-call(f32[24,128]{1,0:T(8,128)} %get-tuple-element.30.trace_ref, f32[8,128]{1,0:T(8,128)} %get-tuple-element.31.state_ref, f32[24,2560]{1,0:T(8,128)} %get-tuple-element.32.faces_ref), custom_call_target="tpu_custom_call" | custom-call | tf_op jit(solution)/shard_map/cond/branch_0_fun/pallas_call | solution.py:813

commit v5 on v4

--- a/solution.py
+++ b/solution.py
@@ -705,7 +705,10 @@
         elements = elements_of(short(split_dot(hot_x[:, 0:32], traces)))
         slots = slots_of(padded(each_element(elements, condensed_ref, 200)))
         start_swap(1 + sweep, slots)
-        start_blocks(1 + 2 * sweep, 3 + 2 * sweep)
+        if sweep == 0:
+            start_blocks(1, 4)
+        else:
+            start_blocks(4, 5)
         if sweep == 0:
             start_stage(2, found)
         total = finish_swap(1 + sweep, slots)

time: 57.2 us -> 55.8 us (0.976)
  Pallas kernels: 55.1 us -> 53.8 us
    pallas_call x1, Pallas kernels: 53.5 us -> 52.2 us  [per_device(): pl.pallas_call(functools.partial(sweep_kernel, doms, subs), out_shape=(ja...]
where the time goes in v5:
time: 55.8 us; the launch traced here: 55.7 us
  Pallas kernels  53.8 us (96%)
  between operations  1.84 us (3%)
    pallas_call x1, Pallas kernels, per_device(): pl.pallas_call(functools.partial(sweep_kernel, doms, subs), out_shape=(ja...  52.2 us
    pallas_call x1, Pallas kernels, finish(): pl.pallas_call(finish_kernel, out_shape=(jax.ShapeDtypeStruct((24, DOF),...  1.63 us

profile of v5, /device:TPU:1, one launch (start us, length us, event | category | flops | bytes accessed | tf_op | source)
XLA Modules:
  0.0 55.7 jit_solution(16418684575552033886)
XLA Ops:
  1.3 52.2 %shard_map.145 = (f32[24,128]{1,0:T(8,128)}, f32[8,128]{1,0:T(8,128)}, f32[24,2560]{1,0:T(8,128)}, s32[1,1]{1,0:T(1,128)}) custom-call(s32[4,8]{1,0:T(4,128)} %bitcast.7, s32[1,2,4]{2,1,0:T(2,128)} %bitcast.9, s32[1,2,4]{2,1,0:T(2,128)} %bitcast.11, s32[1,8]{1,0:T(1,128)} %partner_hbm.1, s32[1]{0:T(128)S(6)} %copy.27.count_hbm, bf16[1,80000]{1,0:T(2,128)(2,1)} %inv_hbm.1, ...), custom_call_target="tpu_custom_call" | custom-call | tf_op jit(solution)/shard_map/pallas_call | solution.py:833
  54.0 1.6 %conditional.1 = ((f32[24,50]{1,0:T(8,128)}, f32[8,100]{1,0:T(8,128)}, bf16[24,2500]{1,0:T(8,128)(2,1)})) conditional(s32[]{:T(128)} %bitcast.6, (f32[24,128]{1,0:T(8,128)}, f32[8,128]{1,0:T(8,128)}, f32[24,2560]{1,0:T(8,128)}) %tuple.13, (s32[8,4]{0,1:T(4,128)}, s32[1,4,2]{1,2,0:T(2,128)}, s32[1,4,2]{1,2,0:T(2,128)}, s32[1,8]{1,0:T(1,128)}, ...), branch_computations={%region_0.0_spmd, %region_1.0_spmd} | conditional | bytes 8 | solution.py:869
  54.0 1.6 %branch_0_fun.1 = (f32[24,50]{1,0:T(8,128)}, f32[8,100]{1,0:T(8,128)}, bf16[24,2500]{1,0:T(8,128)(2,1)}) custom-call(f32[24,128]{1,0:T(8,128)} %get-tuple-element.30.trace_ref, f32[8,128]{1,0:T(8,128)} %get-tuple-element.31.state_ref, f32[24,2560]{1,0:T(8,128)} %get-tuple-element.32.faces_ref), custom_call_target="tpu_custom_call" | custom-call | tf_op jit(solution)/shard_map/cond/branch_0_fun/pallas_call | solution.py:816
